TPU v7x, 32 devices: a whole 2x2x4 slice. The times are simulated.
32 devices in a mesh: row: 8 (over z, x), col: 4 (over y, core).
Axes of the slice: x: 2, y: 2, z: 4, core: 2. Of those that a mesh axis runs over, the one named last changes fastest.
Arguments:
- tile_values: bfloat16 [192, 512, 128], P('row', 'col'), may hold values from -0.0546875 to 0.0546875
- tile_counts: int32 [96, 4], P('row', 'col'), may hold values from 0 to 2, as said below
- tile_cols: int32 [192, 4], P('row', 'col'), may hold values from 0 to 1, as said below
- panels: bfloat16 [12288, 4096], P('row', 'col'), may hold values from -6 to 6
Outputs:
- product: bfloat16 [1024, 4096], P('col', 'row')
Inputs may be any that keep to these rules, and one draw needn't show every extreme that they name: `tile_counts`: within each device the filled slots follow block row order; a device holds at most 24 tiles and some device holds exactly 24 in every draw. `tile_cols`: within one block row of a device the filled slots' columns rise strictly; entries of unfilled slots carry no meaning.
All inputs are finite; a program needn't handle non-finite values.
Results may differ from a plain program's by a relative error of at most 0.001.
Values may be sent and summed in bfloat16 or wider, within the bound.
No kernel may reach another device: no remote copies, remote signals or barrier semaphores. Data moves between devices by JAX's collectives and lax.ppermute only.
A program may use at most 64 MiB of HBM per device.

v0:
```python
import functools

import jax
import jax.numpy as jnp
from jax import lax
from jax.experimental import pallas as pl
from jax.experimental.pallas import tpu as pltpu
from jax.sharding import PartitionSpec as P


GROUPS = 2
SUB = 8
TOP = 32767.0
STEPS = 128.0
VMEM = pl.BlockSpec(memory_space=pltpu.VMEM)
SMEM = pl.BlockSpec(memory_space=pltpu.SMEM)
SMALL = pltpu.CompilerParams(vmem_limit_bytes=16 * 2**20)


def encode(value, ref, at=slice(None)):
    height, width = value.shape
    part = height // GROUPS
    for g in range(GROUPS):
        rows = value[g * part : (g + 1) * part].reshape(part // SUB, SUB, width)
        largest = jnp.max(jnp.abs(rows), axis=0)
        code = jnp.ceil(jnp.log2(jnp.maximum(largest, 1e-30)) * STEPS)
        factor = TOP / jnp.exp2(code / STEPS)
        whole = jnp.clip(jnp.round(rows * factor[None]), -TOP, TOP).astype(jnp.int32)
        ref[g * part : (g + 1) * part, at] = whole.reshape(part, width).astype(jnp.int16)
        whole = code.astype(jnp.int32)
        code_rows = whole if g == 0 else jnp.concatenate([code_rows, whole], 0)
    ref[height : height + GROUPS * SUB, at] = code_rows.astype(jnp.int16)


def decode(coded, height):
    width = coded.shape[1]
    part = height // GROUPS
    codes = coded[height : height + GROUPS * SUB].astype(jnp.int32).astype(jnp.float32)
    pieces = []
    for g in range(GROUPS):
        scale = jnp.exp2(codes[g * SUB : (g + 1) * SUB] / STEPS) * (1.0 / TOP)
        rows = coded[g * part : (g + 1) * part].astype(jnp.int32).astype(jnp.float32)
        pieces.append((rows.reshape(part // SUB, SUB, width) * scale[None]).reshape(part, width))
    return jnp.concatenate(pieces, 0)


def near_memory(value):
    return pltpu.with_memory_space_constraint(value, pltpu.VMEM)


def far_memory(value):
    return pltpu.with_memory_space_constraint(value, pltpu.HBM)


def build_kernel(counts_in, columns_in, tiles_in, *refs):
    outs, (counts, columns, tiles, sems) = refs[:-4], refs[-4:]
    copies = [
        pltpu.make_async_copy(source, target, sems.at[k])
        for k, (source, target) in enumerate(
            ((counts_in, counts), (columns_in, columns), (tiles_in, tiles))
        )
    ]
    for copy in copies:
        copy.start()
    for copy in copies:
        copy.wait()
    tall, wide, slots = counts.shape[0], len(outs), tiles.shape[0]
    edge = tiles.shape[1]
    start = jnp.int32(0)
    for i in range(tall):
        count = counts[i]
        for j, out in enumerate(outs):
            slot, found = jnp.int32(0), jnp.int32(0)
            for t in range(wide):
                at = jnp.minimum(start + t, slots - 1)
                hit = (t < count) & (columns[at] == j)
                slot = jnp.where(hit, at, slot)
                found = jnp.where(hit, 1, found)
            tile = tiles[slot].astype(jnp.float32) * found.astype(jnp.float32)
            out[:, i * edge : (i + 1) * edge] = tile.T.astype(jnp.bfloat16)
        start = start + count


def build(tile_values, tile_counts, tile_cols):
    slots, edge, _ = tile_values.shape
    tall = tile_counts.shape[0]
    return pl.pallas_call(
        build_kernel,
        out_shape=[jax.ShapeDtypeStruct((edge, tall * edge), jnp.bfloat16)] * (slots // tall),
        in_specs=[pl.BlockSpec(memory_space=pltpu.HBM)] * 3,
        out_specs=[VMEM] * (slots // tall),
        scratch_shapes=[
            pltpu.SMEM((tall,), jnp.int32),
            pltpu.SMEM((slots,), jnp.int32),
            pltpu.VMEM(tile_values.shape, tile_values.dtype),
            pltpu.SemaphoreType.DMA((3,)),
        ],
        compiler_params=SMALL,
        name="build",
    )(far_memory(tile_counts[:, 0]), far_memory(tile_cols[:, 0]), far_memory(tile_values))


def product_kernel(place, *refs, count, coded):
    blocks, panels, out = refs[:count], refs[count:-1], refs[-1]
    a = jnp.concatenate([b[...] for b in blocks], 0) if count > 1 else blocks[0][...]
    half = out.shape[1]
    step = min(half, 256)
    start = (1 - place[0] if coded else place[0]) * half
    for n in range(0, half, step):
        at = pl.multiple_of(start + n, step)
        value = jnp.concatenate(
            [jnp.dot(a, b[:, pl.ds(at, step)], preferred_element_type=jnp.float32) for b in panels], 0
        )
        if coded:
            encode(value, out, slice(n, n + step))
        else:
            out[:, n : n + step] = value


def products(place, blocks, panels, half, coded):
    height = len(panels) * len(blocks) * blocks[0].shape[0]
    if coded:
        shape = jax.ShapeDtypeStruct((height + GROUPS * SUB, half), jnp.int16)
    else:
        shape = jax.ShapeDtypeStruct((height, half), jnp.float32)
    return pl.pallas_call(
        functools.partial(product_kernel, count=len(blocks), coded=coded),
        out_shape=shape,
        in_specs=[SMEM] + [VMEM] * (len(blocks) + len(panels)),
        out_specs=VMEM,
        compiler_params=SMALL,
        name="leaving" if coded else "staying",
    )(place, *blocks, *panels)


def coded_shape(height, half):
    return jax.ShapeDtypeStruct((height + GROUPS * SUB, half), jnp.int16)


def split_kernel(place, *refs):
    codeds, kept, hold, send = refs[:-3], refs[-3], refs[-2], refs[-1]
    height = kept.shape[0] // 2
    each = kept.shape[0] // len(codeds)
    value = kept[...] + jnp.concatenate([decode(coded[...], each) for coded in codeds], 0)
    first, second = value[:height], value[height:]
    stays = place[1] == 0
    hold[...] = jnp.where(stays, first, second)
    encode(jnp.where(stays, second, first), send)


def split(place, codeds, kept):
    height, half = kept.shape[0] // 2, kept.shape[1]
    return pl.pallas_call(
        split_kernel,
        out_shape=[jax.ShapeDtypeStruct((height, half), jnp.float32), coded_shape(height, half)],
        in_specs=[SMEM] + [VMEM] * (len(codeds) + 1),
        out_specs=[VMEM, VMEM],
        compiler_params=SMALL,
        name="split",
    )(place, *codeds, kept)


def merge_kernel(coded, kept, *outs):
    value = kept[...] + decode(coded[...], kept.shape[0])
    for hold in outs[:-1]:
        hold[...] = value
    encode(value, outs[-1])


def merge(coded, kept, holds):
    height, half = kept.shape
    out = pl.pallas_call(
        merge_kernel,
        out_shape=[jax.ShapeDtypeStruct((height, half), jnp.float32)] * holds + [coded_shape(height, half)],
        in_specs=[VMEM, VMEM],
        out_specs=[VMEM] * (holds + 1),
        compiler_params=SMALL,
        name="merge",
    )(coded, kept)
    return out if holds else (None, out[0])


def finish_kernel(place, kept, coded, *refs, chunks):
    parts, out = refs[:-1], refs[-1]
    pick = place[2]
    height = out.shape[0] // chunks
    own = kept[...] + decode(coded[...], kept.shape[0])
    for j in range(chunks):
        rows = slice(j * height, (j + 1) * height)
        value = own[rows]
        for k in range(len(parts) // (2 * chunks)):
            at = 2 * (k * chunks + j)
            other = decode(parts[at][...], height) + decode(parts[at + 1][...], height)
            value = jnp.where(pick == k + 1, other, value)
        out[rows] = value.astype(jnp.bfloat16)


def finish(place, kept, coded, parts, chunks):
    return pl.pallas_call(
        functools.partial(finish_kernel, chunks=chunks),
        out_shape=jax.ShapeDtypeStruct(kept.shape, jnp.bfloat16),
        in_specs=[SMEM] + [VMEM] * (2 + len(parts)),
        out_specs=VMEM,
        compiler_params=SMALL,
        name="finish",
    )(place, kept, coded, *parts)


def after(value, *others):
    return lax.optimization_barrier((value, *others))[0]


def solution(mesh):
    rows, cols = mesh.shape["row"], mesh.shape["col"]
    spread = rows // cols
    assert spread == 2 and rows & (rows - 1) == 0 and cols >= 4

    def permute(value, move):
        pairs = [
            (r * cols + c, to[0] * cols + to[1])
            for r in range(rows)
            for c in range(cols)
            if (to := move(r, c)) is not None
        ]
        return lax.ppermute(value, ("row", "col"), pairs)

    last = cols // 2

    last = cols // 2
    inner = last - 2

    def met(r, c, bits):
        return not ((r // spread) ^ c) & bits

    def across(value):
        return permute(value, lambda r, c: (r ^ 1, c))

    def along(value):
        return permute(value, lambda r, c: (r ^ spread, c))

    def folded(got, hold):
        bit = 2
        while bit < last:
            hold, send = merge(got, hold, 1)
            got = permute(
                send,
                lambda r, c: (r ^ (bit * spread), c) if met(r, c, bit - 2) and not met(r, c, bit) else None,
            )
            bit *= 2
        return got, hold

    def body(tile_values, tile_counts, tile_cols, panels):
        half = panels.shape[1] // spread
        r, c = lax.axis_index("row"), lax.axis_index("col")
        q = r // spread
        place = jnp.stack([r % spread, (q + c) % 2, (q ^ c) // 2]).astype(jnp.int32)
        other = near_memory(permute(panels, lambda r, c: (r, c ^ 1)))
        panels = near_memory(panels)

        own = [near_memory(block) for block in build(tile_values, tile_counts, tile_cols)]
        chunks = len(own)
        dense = {0: own}
        bit = last
        while bit > 1:
            for m in list(dense):
                blocks = []
                for j in range(chunks):
                    blocks.append(near_memory(permute(dense[m][j], lambda r, c: (r, c ^ bit))))
                dense[m ^ bit] = blocks
            bit //= 2
        moved = [m for m in sorted(dense) if m]

        first = products(place, own, [panels], half, True)
        sent = [across(first)]
        second = products(place, own, [after(other, first)], half, True)
        sent.append(across(second))
        kept = products(place, own, [after(panels, second), other], half, False)
        coded, stay = {}, {}

        def multiply(j, order):
            for m in moved:
                block = after(dense[m][j], order)
                code = products(place, [block], [panels, other], half, True)
                coded[m, j] = across(code)
                stay[m, j] = products(place, [after(block, code)], [panels, other], half, False)

        multiply(0, kept)
        hold, send = split(place, [sent[0], after(sent[1], stay[moved[0], 0])], kept)
        got = along(send)
        for j in range(1, chunks):
            multiply(j, send)

        parts = {}
        order = send
        for j in range(chunks):
            for m in moved:
                part_hold, part_send = split(place, [after(coded[m, j], order)], stay[m, j])
                part_got, part_hold = folded(along(part_send), part_hold)
                if j == 1:
                    order = part_send
                _, code = merge(part_got, part_hold, 0)
                if j == 0:
                    near = permute(code, lambda r, c: (r, c ^ m) if met(r, c, inner) else None)
                    far = permute(
                        near,
                        lambda r, c: (r ^ (last * spread), c)
                        if met(r, c ^ m, inner) and not met(r, c ^ m, last)
                        else None,
                    )
                else:
                    far = permute(
                        code,
                        lambda r, c: (r ^ (last * spread), c ^ m)
                        if met(r, c, inner) and not met(r, c, last)
                        else None,
                    )
                    near = permute(code, lambda r, c: (r, c ^ m) if met(r, c, inner | last) else None)
                parts[m, j] = [near, far]
        got, hold = folded(got, hold)
        hold, send = merge(got, hold, 1)
        got = permute(
            send,
            lambda r, c: (r ^ (last * spread), c) if met(r, c, inner) and not met(r, c, last) else None,
        )
        pieces = [x for m in moved for j in range(chunks) for x in parts[m, j]]
        return finish(place, hold, got, pieces, chunks)

    return jax.shard_map(
        body,
        mesh=mesh,
        in_specs=(P("row", "col", None), P("row", "col"), P("row", "col"), P("row", "col")),
        out_specs=P("col", "row"),
        check_vma=False,
    )
```

profile of v0, /device:TPU:0, one launch (start us, length us, event | category | flops | bytes accessed | tf_op | source)
XLA Modules:
  0.0 64.6 jit_solution(16983983346164939391)
XLA Ops:
  0.5 2.2 %build.1 = (bf16[128,1536]{1,0:T(8,128)(2,1)}, bf16[128,1536]{1,0:T(8,128)(2,1)S(1)}) custom-call(s32[12]{0:T(128)} %bitcast.5, s32[24]{0:T(128)} %bitcast.6, bf16[24,128,128]{2,1,0:T(8,128)(2,1)} %tiles_in.1), custom_call_target="tpu_custom_call" | custom-call | tf_op jit(solution)/shard_map/build/pallas_call | solution.py:87
  2.7 2.6 %collective-permute-start.3 = (bf16[128,1536]{1,0:T(8,128)(2,1)}, bf16[128,1536]{1,0:T(8,128)(2,1)}, u32[]{:S(2)}, u32[]{:S(2)}) collective-permute-start(bf16[128,1536]{1,0:T(8,128)(2,1)} %get-tuple-element.24.refs_0_), channel_id=1, source_target_pairs={{0,2},{1,3},{2,0},{3,1},{4,6},{5,7},{6,4},{7,5},{8,10},{9,11},{10,... | collective-permute-start | bytes 1179656 | tf_op jit(solution)/shard_map/ppermute | solution.py:225
  5.4 1.9 %copy-done = bf16[1536,1024]{1,0:T(8,128)(2,1)S(1)} copy-done((bf16[1536,1024]{1,0:T(8,128)(2,1)S(1)}, bf16[1536,1024]{1,0:T(8,128)(2,1)}, u32[]{:S(2)}) %copy-start) | copy-done | bytes 3145752
  7.3 1.7 %leaving.4 = s16[272,512]{1,0:T(8,128)(2,1)S(1)} custom-call(s32[3]{0:T(128)S(1)} %pad_add_fusion.place, bf16[128,1536]{1,0:T(8,128)(2,1)} %get-tuple-element.24.refs_0_, bf16[128,1536]{1,0:T(8,128)(2,1)S(1)} %get-tuple-element.25.refs_1_, bf16[1536,1024]{1,0:T(8,128)(2,1)S(1)} %copy-done), custom_call_target="tpu_custom_call" | custom-call | tf_op jit(solution)/shard_map/leaving/pallas_call | solution.py:126
  9.0 1.8 %leaving.5 = s16[272,512]{1,0:T(8,128)(2,1)S(1)} custom-call(s32[3]{0:T(128)S(1)} %pad_add_fusion.place, bf16[128,1536]{1,0:T(8,128)(2,1)} %get-tuple-element.24.refs_0_, bf16[128,1536]{1,0:T(8,128)(2,1)S(1)} %get-tuple-element.25.refs_1_, bf16[1536,1024]{1,0:T(8,128)(2,1)S(1)} %collective-permute-done.1.refs_2_.refs_3_), custom_call_target="tpu_custom_call" | custom-call | tf_op jit(solution)/shard_map/leaving/pallas_call | solution.py:126
  10.9 2.0 %collective-permute-start.2 = (s16[272,512]{1,0:T(8,128)(2,1)S(1)}, s16[272,512]{1,0:T(8,128)(2,1)S(1)}, u32[]{:S(2)}, u32[]{:S(2)}) collective-permute-start(s16[272,512]{1,0:T(8,128)(2,1)S(1)} %leaving.5), channel_id=1, source_target_pairs={{0,4},{1,5},{2,6},{3,7},{4,0},{5,1},{6,2},{7,3},{8,12},{9,13},{10,... | collective-permute-start | bytes 835592 | tf_op jit(solution)/shard_map/ppermute | solution.py:225
  13.0 2.0 %staying.3.refs_2_ = f32[512,512]{1,0:T(8,128)S(1)} custom-call(s32[3]{0:T(128)S(1)} %pad_add_fusion.place, bf16[128,1536]{1,0:T(8,128)(2,1)} %get-tuple-element.24.refs_0_, bf16[128,1536]{1,0:T(8,128)(2,1)S(1)} %get-tuple-element.25.refs_1_, bf16[1536,1024]{1,0:T(8,128)(2,1)S(1)} %copy-done.1, bf16[1536,1024]{1,0:T(8,128)(2,1)S(1)} %collective-permute-done.1.refs_2_.refs_3_), custom_call_target="tpu_custom_call" | custom-call | tf_op jit(solution)/shard_map/staying/pallas_call | solution.py:126
  15.6 1.7 %leaving.6 = s16[272,512]{1,0:T(8,128)(2,1)S(1)} custom-call(s32[3]{0:T(128)S(1)} %pad_add_fusion.place, bf16[128,1536]{1,0:T(8,128)(2,1)} %collective-permute-done.3.refs_0_, bf16[1536,1024]{1,0:T(8,128)(2,1)S(1)} %copy-done.1, bf16[1536,1024]{1,0:T(8,128)(2,1)S(1)} %collective-permute-done.1.refs_2_.refs_3_), custom_call_target="tpu_custom_call" | custom-call | tf_op jit(solution)/shard_map/leaving/pallas_call | solution.py:126
  17.3 2.1 %collective-permute-start.6 = (s16[272,512]{1,0:T(8,128)(2,1)S(1)}, s16[272,512]{1,0:T(8,128)(2,1)S(1)}, u32[]{:S(2)}, u32[]{:S(2)}) collective-permute-start(s16[272,512]{1,0:T(8,128)(2,1)S(1)} %leaving.6), channel_id=1, source_target_pairs={{0,4},{1,5},{2,6},{3,7},{4,0},{5,1},{6,2},{7,3},{8,12},{9,13},{10,... | collective-permute-start | bytes 835592 | tf_op jit(solution)/shard_map/ppermute | solution.py:225
  19.4 1.6 %staying.4.refs_1_ = f32[256,512]{1,0:T(8,128)S(1)} custom-call(s32[3]{0:T(128)S(1)} %pad_add_fusion.place, bf16[128,1536]{1,0:T(8,128)(2,1)} %collective-permute-done.3.refs_0_, bf16[1536,1024]{1,0:T(8,128)(2,1)S(1)} %copy-done.1, bf16[1536,1024]{1,0:T(8,128)(2,1)S(1)} %collective-permute-done.1.refs_2_.refs_3_), custom_call_target="tpu_custom_call" | custom-call | tf_op jit(solution)/shard_map/staying/pallas_call | solution.py:126
  21.0 5.4 %collective-permute-done.refs_0_ = s16[272,512]{1,0:T(8,128)(2,1)S(1)} collective-permute-done((s16[272,512]{1,0:T(8,128)(2,1)S(1)}, s16[272,512]{1,0:T(8,128)(2,1)S(1)}, u32[]{:S(2)}, u32[]{:S(2)}) %collective-permute-start) | collective-permute-done | bytes 278560 | tf_op jit(solution)/shard_map/ppermute | solution.py:225
  27.3 1.8 %leaving.7 = s16[272,512]{1,0:T(8,128)(2,1)S(1)} custom-call(s32[3]{0:T(128)S(1)} %pad_add_fusion.place, bf16[128,1536]{1,0:T(8,128)(2,1)} %collective-permute-done.10.refs_0_, bf16[1536,1024]{1,0:T(8,128)(2,1)S(1)} %copy-done.1, bf16[1536,1024]{1,0:T(8,128)(2,1)S(1)} %collective-permute-done.1.refs_2_.refs_3_), custom_call_target="tpu_custom_call" | custom-call | tf_op jit(solution)/shard_map/leaving/pallas_call | solution.py:126
  29.1 2.0 %collective-permute-start.11 = (s16[272,512]{1,0:T(8,128)(2,1)S(1)}, s16[272,512]{1,0:T(8,128)(2,1)S(1)}, u32[]{:S(2)}, u32[]{:S(2)}) collective-permute-start(s16[272,512]{1,0:T(8,128)(2,1)S(1)} %leaving.7), channel_id=1, source_target_pairs={{0,4},{1,5},{2,6},{3,7},{4,0},{5,1},{6,2},{7,3},{8,12},{9,13},{10,... | collective-permute-start | bytes 835592 | tf_op jit(solution)/shard_map/ppermute | solution.py:225
  31.1 1.6 %collective-permute-start.4 = (s16[272,512]{1,0:T(8,128)(2,1)S(1)}, s16[272,512]{1,0:T(8,128)(2,1)S(1)}, u32[]{:S(2)}, u32[]{:S(2)}) collective-permute-start(s16[272,512]{1,0:T(8,128)(2,1)S(1)} %get-tuple-element.31), channel_id=1, source_target_pairs={{0,8},{1,9},{2,10},{3,11},{4,12},{5,13},{6,14},{7,15},{8,0},{9,1},... | collective-permute-start | bytes 835592 | tf_op jit(solution)/shard_map/ppermute | solution.py:225
  33.3 1.8 %collective-permute-start.7 = (s16[144,512]{1,0:T(8,128)(2,1)S(1)}, s16[144,512]{1,0:T(8,128)(2,1)S(1)}, u32[]{:S(2)}, u32[]{:S(2)}) collective-permute-start(s16[144,512]{1,0:T(8,128)(2,1)S(1)} %get-tuple-element.36), channel_id=1, source_target_pairs={{0,8},{1,9},{2,10},{3,11},{4,12},{5,13},{6,14},{7,15},{8,0},{9,1},... | collective-permute-start | bytes 442376 | tf_op jit(solution)/shard_map/ppermute | solution.py:225
  35.2 1.6 %staying.5.refs_1_ = f32[256,512]{1,0:T(8,128)S(1)} custom-call(s32[3]{0:T(128)S(1)} %pad_add_fusion.place, bf16[128,1536]{1,0:T(8,128)(2,1)} %collective-permute-done.10.refs_0_, bf16[1536,1024]{1,0:T(8,128)(2,1)S(1)} %copy-done.1, bf16[1536,1024]{1,0:T(8,128)(2,1)S(1)} %collective-permute-done.1.refs_2_.refs_3_), custom_call_target="tpu_custom_call" | custom-call | tf_op jit(solution)/shard_map/staying/pallas_call | solution.py:126
  36.8 3.8 %collective-permute-done.7.coded = s16[144,512]{1,0:T(8,128)(2,1)S(1)} collective-permute-done((s16[144,512]{1,0:T(8,128)(2,1)S(1)}, s16[144,512]{1,0:T(8,128)(2,1)S(1)}, u32[]{:S(2)}, u32[]{:S(2)}) %collective-permute-start.7) | collective-permute-done | bytes 147488 | tf_op jit(solution)/shard_map/ppermute | solution.py:225
  40.7 1.6 %collective-permute-start.8 = (s16[144,512]{1,0:T(8,128)(2,1)S(1)}, s16[144,512]{1,0:T(8,128)(2,1)S(1)}, u32[]{:S(2)}, u32[]{:S(2)}) collective-permute-start(s16[144,512]{1,0:T(8,128)(2,1)S(1)} %merge.4), channel_id=1, source_target_pairs={{0,2},{1,3},{2,0},{3,1},{4,6},{5,7},{6,4},{7,5},{8,10},{9,11},{10,... | collective-permute-start | bytes 442376 | tf_op jit(solution)/shard_map/ppermute | solution.py:225
  43.0 1.6 %collective-permute-start.12 = (s16[144,512]{1,0:T(8,128)(2,1)S(1)}, s16[144,512]{1,0:T(8,128)(2,1)S(1)}, u32[]{:S(2)}, u32[]{:S(2)}) collective-permute-start(s16[144,512]{1,0:T(8,128)(2,1)S(1)} %get-tuple-element.41), channel_id=1, source_target_pairs={{0,8},{1,9},{2,10},{3,11},{4,12},{5,13},{6,14},{7,15},{8,0},{9,1},... | collective-permute-start | bytes 442376 | tf_op jit(solution)/shard_map/ppermute | solution.py:225
  44.8 1.3 %collective-permute-start.5 = (s16[272,512]{1,0:T(8,128)(2,1)S(1)}, s16[272,512]{1,0:T(8,128)(2,1)S(1)}, u32[]{:S(2)}, u32[]{:S(2)}) collective-permute-start(s16[272,512]{1,0:T(8,128)(2,1)S(1)} %get-tuple-element.34), channel_id=1, source_target_pairs={{2,18},{3,19},{6,22},{7,23},{10,26},{11,27},{14,30},{15,31},{16,0}... | collective-permute-start | bytes 835592 | tf_op jit(solution)/shard_map/ppermute | solution.py:225
  46.1 5.5 %collective-permute-start.9 = (s16[144,512]{1,0:T(8,128)(2,1)S(1)}, s16[144,512]{1,0:T(8,128)(2,1)S(1)}, u32[]{:S(2)}, u32[]{:S(2)}) collective-permute-start(s16[144,512]{1,0:T(8,128)(2,1)S(1)} %collective-permute-done.8.refs_0_), channel_id=1, source_target_pairs={{0,16},{1,17},{4,20},{5,21},{8,24},{9,25},{12,28},{13,29},{18,2},{... | collective-permute-start | bytes 442376 | tf_op jit(solution)/shard_map/ppermute | solution.py:225
  52.4 4.6 %collective-permute-start.13 = (s16[144,512]{1,0:T(8,128)(2,1)S(1)}, s16[144,512]{1,0:T(8,128)(2,1)S(1)}, u32[]{:S(2)}, u32[]{:S(2)}) collective-permute-start(s16[144,512]{1,0:T(8,128)(2,1)S(1)} %merge.5), channel_id=1, source_target_pairs={{0,2},{1,3},{4,6},{5,7},{8,10},{9,11},{12,14},{13,15},{18,16},{19,... | collective-permute-start | bytes 442376 | tf_op jit(solution)/shard_map/ppermute | solution.py:225
  57.1 6.1 %collective-permute-done.5.coded = s16[272,512]{1,0:T(8,128)(2,1)S(1)} collective-permute-done((s16[272,512]{1,0:T(8,128)(2,1)S(1)}, s16[272,512]{1,0:T(8,128)(2,1)S(1)}, u32[]{:S(2)}, u32[]{:S(2)}) %collective-permute-start.5) | collective-permute-done | bytes 278560 | tf_op jit(solution)/shard_map/ppermute | solution.py:225
  63.1 1.5 %finish.1 = bf16[256,512]{1,0:T(8,128)(2,1)} custom-call(s32[3]{0:T(128)S(1)} %pad_add_fusion.place, f32[256,512]{1,0:T(8,128)S(1)} %get-tuple-element.33.kept, s16[272,512]{1,0:T(8,128)(2,1)S(1)} %collective-permute-done.5.coded, s16[144,512]{1,0:T(8,128)(2,1)S(1)} %collective-permute-done.8.refs_0_, s16[144,512]{1,0:T(8,128)(2,1)S(1)} %collective-permute-done.9.refs_1_, ...), custom_call_target="tpu_custom_call" | custom-call | tf_op jit(solution)/shard_map/finish/pallas_call | solution.py:199
  (26 shorter events, 4.7 us)
Async XLA Ops:
  0.0 9.0 %collective-permute-start.1 = (bf16[1536,1024]{1,0:T(8,128)(2,1)}, bf16[1536,1024]{1,0:T(8,128)(2,1)S(1)}, u32[]{:S(2)}, u32[]{:S(2)}) collective-permute-start(bf16[1536,1024]{1,0:T(8,128)(2,1)} %refs_1_.7), channel_id=1, source_target_pairs={{0,1},{1,0},{2,3},{3,2},{4,5},{5,4},{6,7},{7,6},{8,9},{9,8},{10,11... | collective-permute-start | bytes 9437192 | tf_op jit(solution)/shard_map/ppermute | solution.py:225
  2.7 12.9 %collective-permute-start.3 = (bf16[128,1536]{1,0:T(8,128)(2,1)}, bf16[128,1536]{1,0:T(8,128)(2,1)}, u32[]{:S(2)}, u32[]{:S(2)}) collective-permute-start(bf16[128,1536]{1,0:T(8,128)(2,1)} %get-tuple-element.24.refs_0_), channel_id=1, source_target_pairs={{0,2},{1,3},{2,0},{3,1},{4,6},{5,7},{6,4},{7,5},{8,10},{9,11},{10,... | collective-permute-start | bytes 1179656 | tf_op jit(solution)/shard_map/ppermute | solution.py:225
  5.3 22.0 %collective-permute-start.10 = (bf16[128,1536]{1,0:T(8,128)(2,1)S(1)}, bf16[128,1536]{1,0:T(8,128)(2,1)}, u32[]{:S(2)}, u32[]{:S(2)}) collective-permute-start(bf16[128,1536]{1,0:T(8,128)(2,1)S(1)} %get-tuple-element.25.refs_1_), channel_id=1, source_target_pairs={{0,2},{1,3},{2,0},{3,1},{4,6},{5,7},{6,4},{7,5},{8,10},{9,11},{10,... | collective-permute-start | bytes 1179656 | tf_op jit(solution)/shard_map/ppermute | solution.py:225
  5.4 1.9 %copy-start = (bf16[1536,1024]{1,0:T(8,128)(2,1)S(1)}, bf16[1536,1024]{1,0:T(8,128)(2,1)}, u32[]{:S(2)}) copy-start(bf16[1536,1024]{1,0:T(8,128)(2,1)} %refs_1_.7) | copy-start | bytes 9437188
  9.0 4.0 %copy-start.1 = (bf16[1536,1024]{1,0:T(8,128)(2,1)S(1)}, bf16[1536,1024]{1,0:T(8,128)(2,1)}, u32[]{:S(2)}) copy-start(bf16[1536,1024]{1,0:T(8,128)(2,1)} %refs_1_.7) | copy-start | bytes 9437188
  10.9 10.1 %collective-permute-start.2 = (s16[272,512]{1,0:T(8,128)(2,1)S(1)}, s16[272,512]{1,0:T(8,128)(2,1)S(1)}, u32[]{:S(2)}, u32[]{:S(2)}) collective-permute-start(s16[272,512]{1,0:T(8,128)(2,1)S(1)} %leaving.5), channel_id=1, source_target_pairs={{0,4},{1,5},{2,6},{3,7},{4,0},{5,1},{6,2},{7,3},{8,12},{9,13},{10,... | collective-permute-start | bytes 835592 | tf_op jit(solution)/shard_map/ppermute | solution.py:225
  12.9 13.6 %collective-permute-start = (s16[272,512]{1,0:T(8,128)(2,1)S(1)}, s16[272,512]{1,0:T(8,128)(2,1)S(1)}, u32[]{:S(2)}, u32[]{:S(2)}) collective-permute-start(s16[272,512]{1,0:T(8,128)(2,1)S(1)} %leaving.4), channel_id=1, source_target_pairs={{0,4},{1,5},{2,6},{3,7},{4,0},{5,1},{6,2},{7,3},{8,12},{9,13},{10,... | collective-permute-start | bytes 835592 | tf_op jit(solution)/shard_map/ppermute | solution.py:225
  17.3 15.3 %collective-permute-start.6 = (s16[272,512]{1,0:T(8,128)(2,1)S(1)}, s16[272,512]{1,0:T(8,128)(2,1)S(1)}, u32[]{:S(2)}, u32[]{:S(2)}) collective-permute-start(s16[272,512]{1,0:T(8,128)(2,1)S(1)} %leaving.6), channel_id=1, source_target_pairs={{0,4},{1,5},{2,6},{3,7},{4,0},{5,1},{6,2},{7,3},{8,12},{9,13},{10,... | collective-permute-start | bytes 835592 | tf_op jit(solution)/shard_map/ppermute | solution.py:225
  29.1 13.2 %collective-permute-start.11 = (s16[272,512]{1,0:T(8,128)(2,1)S(1)}, s16[272,512]{1,0:T(8,128)(2,1)S(1)}, u32[]{:S(2)}, u32[]{:S(2)}) collective-permute-start(s16[272,512]{1,0:T(8,128)(2,1)S(1)} %leaving.7), channel_id=1, source_target_pairs={{0,4},{1,5},{2,6},{3,7},{4,0},{5,1},{6,2},{7,3},{8,12},{9,13},{10,... | collective-permute-start | bytes 835592 | tf_op jit(solution)/shard_map/ppermute | solution.py:225
  31.1 13.6 %collective-permute-start.4 = (s16[272,512]{1,0:T(8,128)(2,1)S(1)}, s16[272,512]{1,0:T(8,128)(2,1)S(1)}, u32[]{:S(2)}, u32[]{:S(2)}) collective-permute-start(s16[272,512]{1,0:T(8,128)(2,1)S(1)} %get-tuple-element.31), channel_id=1, source_target_pairs={{0,8},{1,9},{2,10},{3,11},{4,12},{5,13},{6,14},{7,15},{8,0},{9,1},... | collective-permute-start | bytes 835592 | tf_op jit(solution)/shard_map/ppermute | solution.py:225
  33.3 7.2 %collective-permute-start.7 = (s16[144,512]{1,0:T(8,128)(2,1)S(1)}, s16[144,512]{1,0:T(8,128)(2,1)S(1)}, u32[]{:S(2)}, u32[]{:S(2)}) collective-permute-start(s16[144,512]{1,0:T(8,128)(2,1)S(1)} %get-tuple-element.36), channel_id=1, source_target_pairs={{0,8},{1,9},{2,10},{3,11},{4,12},{5,13},{6,14},{7,15},{8,0},{9,1},... | collective-permute-start | bytes 442376 | tf_op jit(solution)/shard_map/ppermute | solution.py:225
  40.7 5.4 %collective-permute-start.8 = (s16[144,512]{1,0:T(8,128)(2,1)S(1)}, s16[144,512]{1,0:T(8,128)(2,1)S(1)}, u32[]{:S(2)}, u32[]{:S(2)}) collective-permute-start(s16[144,512]{1,0:T(8,128)(2,1)S(1)} %merge.4), channel_id=1, source_target_pairs={{0,2},{1,3},{2,0},{3,1},{4,6},{5,7},{6,4},{7,5},{8,10},{9,11},{10,... | collective-permute-start | bytes 442376 | tf_op jit(solution)/shard_map/ppermute | solution.py:225
  43.0 8.6 %collective-permute-start.12 = (s16[144,512]{1,0:T(8,128)(2,1)S(1)}, s16[144,512]{1,0:T(8,128)(2,1)S(1)}, u32[]{:S(2)}, u32[]{:S(2)}) collective-permute-start(s16[144,512]{1,0:T(8,128)(2,1)S(1)} %get-tuple-element.41), channel_id=1, source_target_pairs={{0,8},{1,9},{2,10},{3,11},{4,12},{5,13},{6,14},{7,15},{8,0},{9,1},... | collective-permute-start | bytes 442376 | tf_op jit(solution)/shard_map/ppermute | solution.py:225
  44.8 18.3 %collective-permute-start.5 = (s16[272,512]{1,0:T(8,128)(2,1)S(1)}, s16[272,512]{1,0:T(8,128)(2,1)S(1)}, u32[]{:S(2)}, u32[]{:S(2)}) collective-permute-start(s16[272,512]{1,0:T(8,128)(2,1)S(1)} %get-tuple-element.34), channel_id=1, source_target_pairs={{2,18},{3,19},{6,22},{7,23},{10,26},{11,27},{14,30},{15,31},{16,0}... | collective-permute-start | bytes 835592 | tf_op jit(solution)/shard_map/ppermute | solution.py:225
  46.1 10.9 %collective-permute-start.9 = (s16[144,512]{1,0:T(8,128)(2,1)S(1)}, s16[144,512]{1,0:T(8,128)(2,1)S(1)}, u32[]{:S(2)}, u32[]{:S(2)}) collective-permute-start(s16[144,512]{1,0:T(8,128)(2,1)S(1)} %collective-permute-done.8.refs_0_), channel_id=1, source_target_pairs={{0,16},{1,17},{4,20},{5,21},{8,24},{9,25},{12,28},{13,29},{18,2},{... | collective-permute-start | bytes 442376 | tf_op jit(solution)/shard_map/ppermute | solution.py:225
  51.7 11.4 %collective-permute-start.14 = (s16[144,512]{1,0:T(8,128)(2,1)S(1)}, s16[144,512]{1,0:T(8,128)(2,1)S(1)}, u32[]{:S(2)}, u32[]{:S(2)}) collective-permute-start(s16[144,512]{1,0:T(8,128)(2,1)S(1)} %merge.5), channel_id=1, source_target_pairs={{2,16},{3,17},{6,20},{7,21},{10,24},{11,25},{14,28},{15,29},{16,2}... | collective-permute-start | bytes 442376 | tf_op jit(solution)/shard_map/ppermute | solution.py:225
  52.4 10.7 %collective-permute-start.13 = (s16[144,512]{1,0:T(8,128)(2,1)S(1)}, s16[144,512]{1,0:T(8,128)(2,1)S(1)}, u32[]{:S(2)}, u32[]{:S(2)}) collective-permute-start(s16[144,512]{1,0:T(8,128)(2,1)S(1)} %merge.5), channel_id=1, source_target_pairs={{0,2},{1,3},{4,6},{5,7},{8,10},{9,11},{12,14},{13,15},{18,16},{19,... | collective-permute-start | bytes 442376 | tf_op jit(solution)/shard_map/ppermute | solution.py:225
where the time goes:
time: 65.2 us; the launch traced here: 64.6 us
  starting transfers between devices  28 us (43%)
  Pallas kernels  18.6 us (29%)
  waiting for transfers between devices  15.9 us (24%)
  local copies, waits for them, and re-layouts  1.9 us (3%)
    ppermute x15, starting transfers between devices, permute(): return lax.ppermute(value, ('row', 'col'), pairs)  28 us
    ppermute x15, waiting for transfers between devices, permute(): return lax.ppermute(value, ('row', 'col'), pairs)  15.9 us
    pallas_call x7, Pallas kernels, products(): pl.pallas_call(functools.partial(product_kernel, count=len(blocks), coded...  12.3 us
    pallas_call x3, Pallas kernels, split(): pl.pallas_call(split_kernel, out_shape=[jax.ShapeDtypeStruct((height, hal...  2.25 us
    pallas_call x1, Pallas kernels, build(): pl.pallas_call(build_kernel, out_shape=[jax.ShapeDtypeStruct((edge, tall...  2.2 us
    unnamed x4, local copies, waits for them, and re-layouts  1.9 us
    pallas_call x1, Pallas kernels, finish(): pl.pallas_call(functools.partial(finish_kernel, chunks=chunks), out_shape...  1.48 us
  transfers between devices with their start and end apart: 15, of which 4 were waited for; matrix products, arithmetic and copies ran while one was open for 0% of the time, Pallas kernels for 27%

commit v1 on v0

--- a/solution.py
+++ b/solution.py
@@ -13,7 +13,6 @@
 TOP = 32767.0
 STEPS = 128.0
 VMEM = pl.BlockSpec(memory_space=pltpu.VMEM)
-SMEM = pl.BlockSpec(memory_space=pltpu.SMEM)
 SMALL = pltpu.CompilerParams(vmem_limit_bytes=16 * 2**20)
 
 
@@ -44,6 +43,12 @@
     return jnp.concatenate(pieces, 0)
 
 
+def places(spread):
+    r, c = lax.axis_index("row"), lax.axis_index("col")
+    q = r // spread
+    return r % spread, (q + c) % 2, (q // 2) ^ (c // 2)
+
+
 def near_memory(value):
     return pltpu.with_memory_space_constraint(value, pltpu.VMEM)
 
@@ -52,17 +57,17 @@
     return pltpu.with_memory_space_constraint(value, pltpu.HBM)
 
 
-def build_kernel(counts_in, columns_in, tiles_in, *refs):
-    outs, (counts, columns, tiles, sems) = refs[:-4], refs[-4:]
+def build_kernel(counts_in, columns_in, tiles_in, panels_in, *refs):
+    outs, (panels, counts, columns, tiles, sems) = refs[:-5], refs[-5:]
     copies = [
         pltpu.make_async_copy(source, target, sems.at[k])
         for k, (source, target) in enumerate(
-            ((counts_in, counts), (columns_in, columns), (tiles_in, tiles))
+            ((counts_in, counts), (columns_in, columns), (tiles_in, tiles), (panels_in, panels))
         )
     ]
     for copy in copies:
         copy.start()
-    for copy in copies:
+    for copy in copies[:-1]:
         copy.wait()
     tall, wide, slots = counts.shape[0], len(outs), tiles.shape[0]
     edge = tiles.shape[1]
@@ -79,33 +84,36 @@
             tile = tiles[slot].astype(jnp.float32) * found.astype(jnp.float32)
             out[:, i * edge : (i + 1) * edge] = tile.T.astype(jnp.bfloat16)
         start = start + count
-
-
-def build(tile_values, tile_counts, tile_cols):
+    copies[-1].wait()
+
+
+def build(tile_values, tile_counts, tile_cols, panels):
     slots, edge, _ = tile_values.shape
     tall = tile_counts.shape[0]
     return pl.pallas_call(
         build_kernel,
-        out_shape=[jax.ShapeDtypeStruct((edge, tall * edge), jnp.bfloat16)] * (slots // tall),
-        in_specs=[pl.BlockSpec(memory_space=pltpu.HBM)] * 3,
-        out_specs=[VMEM] * (slots // tall),
+        out_shape=[jax.ShapeDtypeStruct((edge, tall * edge), jnp.bfloat16)] * (slots // tall)
+        + [jax.ShapeDtypeStruct(panels.shape, panels.dtype)],
+        in_specs=[pl.BlockSpec(memory_space=pltpu.HBM)] * 4,
+        out_specs=[VMEM] * (slots // tall + 1),
         scratch_shapes=[
             pltpu.SMEM((tall,), jnp.int32),
             pltpu.SMEM((slots,), jnp.int32),
             pltpu.VMEM(tile_values.shape, tile_values.dtype),
-            pltpu.SemaphoreType.DMA((3,)),
+            pltpu.SemaphoreType.DMA((4,)),
         ],
         compiler_params=SMALL,
         name="build",
-    )(far_memory(tile_counts[:, 0]), far_memory(tile_cols[:, 0]), far_memory(tile_values))
-
-
-def product_kernel(place, *refs, count, coded):
+    )(far_memory(tile_counts[:, 0]), far_memory(tile_cols[:, 0]), far_memory(tile_values), far_memory(panels))
+
+
+def product_kernel(*refs, count, coded, spread):
     blocks, panels, out = refs[:count], refs[count:-1], refs[-1]
     a = jnp.concatenate([b[...] for b in blocks], 0) if count > 1 else blocks[0][...]
     half = out.shape[1]
     step = min(half, 256)
-    start = (1 - place[0] if coded else place[0]) * half
+    side = places(spread)[0]
+    start = (1 - side if coded else side) * half
     for n in range(0, half, step):
         at = pl.multiple_of(start + n, step)
         value = jnp.concatenate(
@@ -117,47 +125,49 @@
             out[:, n : n + step] = value
 
 
-def products(place, blocks, panels, half, coded):
+def products(blocks, panels, half, coded):
     height = len(panels) * len(blocks) * blocks[0].shape[0]
     if coded:
         shape = jax.ShapeDtypeStruct((height + GROUPS * SUB, half), jnp.int16)
     else:
         shape = jax.ShapeDtypeStruct((height, half), jnp.float32)
     return pl.pallas_call(
-        functools.partial(product_kernel, count=len(blocks), coded=coded),
+        functools.partial(
+            product_kernel, count=len(blocks), coded=coded, spread=panels[0].shape[1] // half
+        ),
         out_shape=shape,
-        in_specs=[SMEM] + [VMEM] * (len(blocks) + len(panels)),
+        in_specs=[VMEM] * (len(blocks) + len(panels)),
         out_specs=VMEM,
         compiler_params=SMALL,
         name="leaving" if coded else "staying",
-    )(place, *blocks, *panels)
+    )(*blocks, *panels)
 
 
 def coded_shape(height, half):
     return jax.ShapeDtypeStruct((height + GROUPS * SUB, half), jnp.int16)
 
 
-def split_kernel(place, *refs):
+def split_kernel(*refs, spread):
     codeds, kept, hold, send = refs[:-3], refs[-3], refs[-2], refs[-1]
     height = kept.shape[0] // 2
     each = kept.shape[0] // len(codeds)
     value = kept[...] + jnp.concatenate([decode(coded[...], each) for coded in codeds], 0)
     first, second = value[:height], value[height:]
-    stays = place[1] == 0
+    stays = places(spread)[1] == 0
     hold[...] = jnp.where(stays, first, second)
     encode(jnp.where(stays, second, first), send)
 
 
-def split(place, codeds, kept):
+def split(codeds, kept, spread):
     height, half = kept.shape[0] // 2, kept.shape[1]
     return pl.pallas_call(
-        split_kernel,
+        functools.partial(split_kernel, spread=spread),
         out_shape=[jax.ShapeDtypeStruct((height, half), jnp.float32), coded_shape(height, half)],
-        in_specs=[SMEM] + [VMEM] * (len(codeds) + 1),
+        in_specs=[VMEM] * (len(codeds) + 1),
         out_specs=[VMEM, VMEM],
         compiler_params=SMALL,
         name="split",
-    )(place, *codeds, kept)
+    )(*codeds, kept)
 
 
 def merge_kernel(coded, kept, *outs):
@@ -180,9 +190,9 @@
     return out if holds else (None, out[0])
 
 
-def finish_kernel(place, kept, coded, *refs, chunks):
+def finish_kernel(kept, coded, *refs, chunks, spread):
     parts, out = refs[:-1], refs[-1]
-    pick = place[2]
+    pick = places(spread)[2]
     height = out.shape[0] // chunks
     own = kept[...] + decode(coded[...], kept.shape[0])
     for j in range(chunks):
@@ -195,15 +205,15 @@
         out[rows] = value.astype(jnp.bfloat16)
 
 
-def finish(place, kept, coded, parts, chunks):
+def finish(kept, coded, parts, chunks, spread):
     return pl.pallas_call(
-        functools.partial(finish_kernel, chunks=chunks),
+        functools.partial(finish_kernel, chunks=chunks, spread=spread),
         out_shape=jax.ShapeDtypeStruct(kept.shape, jnp.bfloat16),
-        in_specs=[SMEM] + [VMEM] * (2 + len(parts)),
+        in_specs=[VMEM] * (2 + len(parts)),
         out_specs=VMEM,
         compiler_params=SMALL,
         name="finish",
-    )(place, kept, coded, *parts)
+    )(kept, coded, *parts)
 
 
 def after(value, *others):
@@ -251,13 +261,8 @@
 
     def body(tile_values, tile_counts, tile_cols, panels):
         half = panels.shape[1] // spread
-        r, c = lax.axis_index("row"), lax.axis_index("col")
-        q = r // spread
-        place = jnp.stack([r % spread, (q + c) % 2, (q ^ c) // 2]).astype(jnp.int32)
         other = near_memory(permute(panels, lambda r, c: (r, c ^ 1)))
-        panels = near_memory(panels)
-
-        own = [near_memory(block) for block in build(tile_values, tile_counts, tile_cols)]
+        *own, panels = [near_memory(x) for x in build(tile_values, tile_counts, tile_cols, panels)]
         chunks = len(own)
         dense = {0: own}
         bit = last
@@ -270,35 +275,43 @@
             bit //= 2
         moved = [m for m in sorted(dense) if m]
 
-        first = products(place, own, [panels], half, True)
+        first = products(own, [panels], half, True)
         sent = [across(first)]
-        second = products(place, own, [after(other, first)], half, True)
+        second = products(own, [after(other, first)], half, True)
         sent.append(across(second))
-        kept = products(place, own, [after(panels, second), other], half, False)
+        kept = products(own, [after(panels, second), other], half, False)
         coded, stay = {}, {}
 
         def multiply(j, order):
             for m in moved:
                 block = after(dense[m][j], order)
-                code = products(place, [block], [panels, other], half, True)
+                code = products([block], [panels, other], half, True)
                 coded[m, j] = across(code)
-                stay[m, j] = products(place, [after(block, code)], [panels, other], half, False)
+                stay[m, j] = products([after(block, code)], [panels, other], half, False)
 
         multiply(0, kept)
-        hold, send = split(place, [sent[0], after(sent[1], stay[moved[0], 0])], kept)
+        hold, send = split([sent[0], after(sent[1], stay[moved[0], 0])], kept, spread)
         got = along(send)
         for j in range(1, chunks):
             multiply(j, send)
 
         parts = {}
-        order = send
+        order = stay[moved[-1], chunks - 1]
         for j in range(chunks):
             for m in moved:
-                part_hold, part_send = split(place, [after(coded[m, j], order)], stay[m, j])
+                part_hold, part_send = split([after(coded[m, j], order)], stay[m, j], spread)
                 part_got, part_hold = folded(along(part_send), part_hold)
-                if j == 1:
-                    order = part_send
-                _, code = merge(part_got, part_hold, 0)
+                if j == 0 and m == moved[0]:
+                    got, hold = folded(got, hold)
+                    hold, send = merge(after(got, part_send), hold, 1)
+                    got = permute(
+                        send,
+                        lambda r, c: (r ^ (last * spread), c)
+                        if met(r, c, inner) and not met(r, c, last)
+                        else None,
+                    )
+                _, code = merge(after(part_got, send), part_hold, 0)
+                order = code
                 if j == 0:
                     near = permute(code, lambda r, c: (r, c ^ m) if met(r, c, inner) else None)
                     far = permute(
@@ -316,14 +329,8 @@
                     )
                     near = permute(code, lambda r, c: (r, c ^ m) if met(r, c, inner | last) else None)
                 parts[m, j] = [near, far]
-        got, hold = folded(got, hold)
-        hold, send = merge(got, hold, 1)
-        got = permute(
-            send,
-            lambda r, c: (r ^ (last * spread), c) if met(r, c, inner) and not met(r, c, last) else None,
-        )
         pieces = [x for m in moved for j in range(chunks) for x in parts[m, j]]
-        return finish(place, hold, got, pieces, chunks)
+        return finish(hold, got, pieces, chunks, spread)
 
     return jax.shard_map(
         body,

time: 65.2 us -> 59.9 us (0.919)
  the two profiles are of different devices: /device:TPU:0 before, /device:TPU:4 now
where the time goes in v1:
time: 59.9 us; the launch traced here: 59.7 us
  waiting for transfers between devices  26.9 us (45%)
  starting transfers between devices  23.3 us (39%)
  Pallas kernels  9.3 us (16%)
    ppermute x15, waiting for transfers between devices, permute(): return lax.ppermute(value, ('row', 'col'), pairs)  26.9 us
    ppermute x15, starting transfers between devices, permute(): return lax.ppermute(value, ('row', 'col'), pairs)  23.3 us
    pallas_call x7, Pallas kernels, products(): pl.pallas_call(functools.partial(product_kernel, count=len(blocks), coded...  5.14 us
    pallas_call x1, Pallas kernels, build(): pl.pallas_call(build_kernel, out_shape=[jax.ShapeDtypeStruct((edge, tall...  2.17 us
  transfers between devices with their start and end apart: 15, of which 6 were waited for; matrix products, arithmetic and copies ran while one was open for 0% of the time, Pallas kernels for 14%

profile of v1, /device:TPU:4, one launch (start us, length us, event | category | flops | bytes accessed | tf_op | source)
XLA Modules:
  0.0 59.7 jit_solution(12779932137997711996)
XLA Ops:
  0.0 2.2 %build.1 = (bf16[128,1536]{1,0:T(8,128)(2,1)S(1)}, bf16[128,1536]{1,0:T(8,128)(2,1)S(1)}, bf16[1536,1024]{1,0:T(8,128)(2,1)S(1)}) custom-call(s32[12]{0:T(128)} %bitcast.2, s32[24]{0:T(128)} %bitcast.3, bf16[24,128,128]{2,1,0:T(8,128)(2,1)} %tiles_in.1, bf16[1536,1024]{1,0:T(8,128)(2,1)} %panels_in.1), custom_call_target="tpu_custom_call" | custom-call | tf_op jit(solution)/shard_map/build/pallas_call | solution.py:93
  2.3 2.0 %collective-permute-start.6 = (bf16[128,1536]{1,0:T(8,128)(2,1)S(1)}, bf16[128,1536]{1,0:T(8,128)(2,1)S(1)}, u32[]{:S(2)}, u32[]{:S(2)}) collective-permute-start(bf16[128,1536]{1,0:T(8,128)(2,1)S(1)} %get-tuple-element.29.refs_1_), channel_id=1, source_target_pairs={{0,2},{1,3},{2,0},{3,1},{4,6},{5,7},{6,4},{7,5},{8,10},{9,11},{10,... | collective-permute-start | bytes 1179656 | tf_op jit(solution)/shard_map/ppermute | solution.py:235
  4.3 0.7 %leaving.4 = s16[272,512]{1,0:T(8,128)(2,1)S(1)} custom-call(bf16[128,1536]{1,0:T(8,128)(2,1)S(1)} %get-tuple-element.28.refs_0_, bf16[128,1536]{1,0:T(8,128)(2,1)S(1)} %get-tuple-element.29.refs_1_, bf16[1536,1024]{1,0:T(8,128)(2,1)S(1)} %get-tuple-element.32.refs_2_.refs_1_), custom_call_target="tpu_custom_call" | custom-call | tf_op jit(solution)/shard_map/leaving/pallas_call | solution.py:134
  5.0 0.9 %collective-permute-done.1.refs_2_.refs_3_ = bf16[1536,1024]{1,0:T(8,128)(2,1)S(1)} collective-permute-done((bf16[1536,1024]{1,0:T(8,128)(2,1)}, bf16[1536,1024]{1,0:T(8,128)(2,1)S(1)}, u32[]{:S(2)}, u32[]{:S(2)}) %collective-permute-start.1) | collective-permute-done | bytes 3145760 | tf_op jit(solution)/shard_map/ppermute | solution.py:235
  5.9 0.7 %leaving.5 = s16[272,512]{1,0:T(8,128)(2,1)S(1)} custom-call(bf16[128,1536]{1,0:T(8,128)(2,1)S(1)} %get-tuple-element.28.refs_0_, bf16[128,1536]{1,0:T(8,128)(2,1)S(1)} %get-tuple-element.29.refs_1_, bf16[1536,1024]{1,0:T(8,128)(2,1)S(1)} %collective-permute-done.1.refs_2_.refs_3_), custom_call_target="tpu_custom_call" | custom-call | tf_op jit(solution)/shard_map/leaving/pallas_call | solution.py:134
  6.5 1.6 %collective-permute-start.2 = (s16[272,512]{1,0:T(8,128)(2,1)S(1)}, s16[272,512]{1,0:T(8,128)(2,1)S(1)}, u32[]{:S(2)}, u32[]{:S(2)}) collective-permute-start(s16[272,512]{1,0:T(8,128)(2,1)S(1)} %leaving.5), channel_id=1, source_target_pairs={{0,4},{1,5},{2,6},{3,7},{4,0},{5,1},{6,2},{7,3},{8,12},{9,13},{10,... | collective-permute-start | bytes 835592 | tf_op jit(solution)/shard_map/ppermute | solution.py:235
  8.6 1.0 %staying.3.refs_2_ = f32[512,512]{1,0:T(8,128)S(1)} custom-call(bf16[128,1536]{1,0:T(8,128)(2,1)S(1)} %get-tuple-element.28.refs_0_, bf16[128,1536]{1,0:T(8,128)(2,1)S(1)} %get-tuple-element.29.refs_1_, bf16[1536,1024]{1,0:T(8,128)(2,1)S(1)} %get-tuple-element.32.refs_2_.refs_1_, bf16[1536,1024]{1,0:T(8,128)(2,1)S(1)} %collective-permute-done.1.refs_2_.refs_3_), custom_call_target="tpu_custom_call" | custom-call | tf_op jit(solution)/shard_map/staying/pallas_call | solution.py:134
  9.6 4.6 %collective-permute-done.3.refs_0_ = bf16[128,1536]{1,0:T(8,128)(2,1)S(1)} collective-permute-done((bf16[128,1536]{1,0:T(8,128)(2,1)S(1)}, bf16[128,1536]{1,0:T(8,128)(2,1)S(1)}, u32[]{:S(2)}, u32[]{:S(2)}) %collective-permute-start.3) | collective-permute-done | bytes 393248 | tf_op jit(solution)/shard_map/ppermute | solution.py:235
  14.2 0.8 %leaving.6 = s16[272,512]{1,0:T(8,128)(2,1)S(1)} custom-call(bf16[128,1536]{1,0:T(8,128)(2,1)S(1)} %collective-permute-done.3.refs_0_, bf16[1536,1024]{1,0:T(8,128)(2,1)S(1)} %get-tuple-element.32.refs_2_.refs_1_, bf16[1536,1024]{1,0:T(8,128)(2,1)S(1)} %collective-permute-done.1.refs_2_.refs_3_), custom_call_target="tpu_custom_call" | custom-call | tf_op jit(solution)/shard_map/leaving/pallas_call | solution.py:134
  15.0 1.5 %collective-permute-start.5 = (s16[272,512]{1,0:T(8,128)(2,1)S(1)}, s16[272,512]{1,0:T(8,128)(2,1)S(1)}, u32[]{:S(2)}, u32[]{:S(2)}) collective-permute-start(s16[272,512]{1,0:T(8,128)(2,1)S(1)} %leaving.6), channel_id=1, source_target_pairs={{0,4},{1,5},{2,6},{3,7},{4,0},{5,1},{6,2},{7,3},{8,12},{9,13},{10,... | collective-permute-start | bytes 835592 | tf_op jit(solution)/shard_map/ppermute | solution.py:235
  17.2 4.9 %collective-permute-done.refs_0_ = s16[272,512]{1,0:T(8,128)(2,1)S(1)} collective-permute-done((s16[272,512]{1,0:T(8,128)(2,1)S(1)}, s16[272,512]{1,0:T(8,128)(2,1)S(1)}, u32[]{:S(2)}, u32[]{:S(2)}) %collective-permute-start) | collective-permute-done | bytes 278560 | tf_op jit(solution)/shard_map/ppermute | solution.py:235
  22.4 1.6 %collective-permute-start.4 = (s16[272,512]{1,0:T(8,128)(2,1)S(1)}, s16[272,512]{1,0:T(8,128)(2,1)S(1)}, u32[]{:S(2)}, u32[]{:S(2)}) collective-permute-start(s16[272,512]{1,0:T(8,128)(2,1)S(1)} %get-tuple-element.36), channel_id=1, source_target_pairs={{0,8},{1,9},{2,10},{3,11},{4,12},{5,13},{6,14},{7,15},{8,0},{9,1},... | collective-permute-start | bytes 835592 | tf_op jit(solution)/shard_map/ppermute | solution.py:235
  24.1 0.8 %leaving.7 = s16[272,512]{1,0:T(8,128)(2,1)S(1)} custom-call(bf16[128,1536]{1,0:T(8,128)(2,1)S(1)} %collective-permute-done.6.refs_0_, bf16[1536,1024]{1,0:T(8,128)(2,1)S(1)} %get-tuple-element.32.refs_2_.refs_1_, bf16[1536,1024]{1,0:T(8,128)(2,1)S(1)} %collective-permute-done.1.refs_2_.refs_3_), custom_call_target="tpu_custom_call" | custom-call | tf_op jit(solution)/shard_map/leaving/pallas_call | solution.py:134
  24.8 1.6 %collective-permute-start.11 = (s16[272,512]{1,0:T(8,128)(2,1)S(1)}, s16[272,512]{1,0:T(8,128)(2,1)S(1)}, u32[]{:S(2)}, u32[]{:S(2)}) collective-permute-start(s16[272,512]{1,0:T(8,128)(2,1)S(1)} %leaving.7), channel_id=1, source_target_pairs={{0,4},{1,5},{2,6},{3,7},{4,0},{5,1},{6,2},{7,3},{8,12},{9,13},{10,... | collective-permute-start | bytes 835592 | tf_op jit(solution)/shard_map/ppermute | solution.py:235
  27.0 1.0 %collective-permute-done.5.refs_0_ = s16[272,512]{1,0:T(8,128)(2,1)S(1)} collective-permute-done((s16[272,512]{1,0:T(8,128)(2,1)S(1)}, s16[272,512]{1,0:T(8,128)(2,1)S(1)}, u32[]{:S(2)}, u32[]{:S(2)}) %collective-permute-start.5) | collective-permute-done | bytes 278560 | tf_op jit(solution)/shard_map/ppermute | solution.py:235
  28.2 1.6 %collective-permute-start.8 = (s16[144,512]{1,0:T(8,128)(2,1)S(1)}, s16[144,512]{1,0:T(8,128)(2,1)S(1)}, u32[]{:S(2)}, u32[]{:S(2)}) collective-permute-start(s16[144,512]{1,0:T(8,128)(2,1)S(1)} %get-tuple-element.40), channel_id=1, source_target_pairs={{0,8},{1,9},{2,10},{3,11},{4,12},{5,13},{6,14},{7,15},{8,0},{9,1},... | collective-permute-start | bytes 442376 | tf_op jit(solution)/shard_map/ppermute | solution.py:235
  30.1 3.4 %collective-permute-done.8.coded = s16[144,512]{1,0:T(8,128)(2,1)S(1)} collective-permute-done((s16[144,512]{1,0:T(8,128)(2,1)S(1)}, s16[144,512]{1,0:T(8,128)(2,1)S(1)}, u32[]{:S(2)}, u32[]{:S(2)}) %collective-permute-start.8) | collective-permute-done | bytes 147488 | tf_op jit(solution)/shard_map/ppermute | solution.py:235
  33.8 1.6 %collective-permute-start.12 = (s16[144,512]{1,0:T(8,128)(2,1)S(1)}, s16[144,512]{1,0:T(8,128)(2,1)S(1)}, u32[]{:S(2)}, u32[]{:S(2)}) collective-permute-start(s16[144,512]{1,0:T(8,128)(2,1)S(1)} %get-tuple-element.48), channel_id=1, source_target_pairs={{0,8},{1,9},{2,10},{3,11},{4,12},{5,13},{6,14},{7,15},{8,0},{9,1},... | collective-permute-start | bytes 442376 | tf_op jit(solution)/shard_map/ppermute | solution.py:235
  35.9 4.5 %collective-permute-start.7 = (s16[272,512]{1,0:T(8,128)(2,1)S(1)}, s16[272,512]{1,0:T(8,128)(2,1)S(1)}, u32[]{:S(2)}, u32[]{:S(2)}) collective-permute-start(s16[272,512]{1,0:T(8,128)(2,1)S(1)} %get-tuple-element.44), channel_id=1, source_target_pairs={{2,18},{3,19},{6,22},{7,23},{10,26},{11,27},{14,30},{15,31},{16,0}... | collective-permute-start | bytes 835592 | tf_op jit(solution)/shard_map/ppermute | solution.py:235
  40.5 3.5 %collective-permute-start.14 = (s16[144,512]{1,0:T(8,128)(2,1)S(1)}, s16[144,512]{1,0:T(8,128)(2,1)S(1)}, u32[]{:S(2)}, u32[]{:S(2)}) collective-permute-start(s16[144,512]{1,0:T(8,128)(2,1)S(1)} %merge.5), channel_id=1, source_target_pairs={{2,16},{3,17},{6,20},{7,21},{10,24},{11,25},{14,28},{15,29},{16,2}... | collective-permute-start | bytes 442376 | tf_op jit(solution)/shard_map/ppermute | solution.py:235
  44.1 1.3 %collective-permute-start.13 = (s16[144,512]{1,0:T(8,128)(2,1)S(1)}, s16[144,512]{1,0:T(8,128)(2,1)S(1)}, u32[]{:S(2)}, u32[]{:S(2)}) collective-permute-start(s16[144,512]{1,0:T(8,128)(2,1)S(1)} %merge.5), channel_id=1, source_target_pairs={{0,2},{1,3},{4,6},{5,7},{8,10},{9,11},{12,14},{13,15},{18,16},{19,... | collective-permute-start | bytes 442376 | tf_op jit(solution)/shard_map/ppermute | solution.py:235
  45.4 1.3 %collective-permute-start.10 = (s16[144,512]{1,0:T(8,128)(2,1)S(1)}, s16[144,512]{1,0:T(8,128)(2,1)S(1)}, u32[]{:S(2)}, u32[]{:S(2)}) collective-permute-start(s16[144,512]{1,0:T(8,128)(2,1)S(1)} %collective-permute-done.9.refs_0_), channel_id=1, source_target_pairs={{0,16},{1,17},{4,20},{5,21},{8,24},{9,25},{12,28},{13,29},{18,2},{... | collective-permute-start | bytes 442376 | tf_op jit(solution)/shard_map/ppermute | solution.py:235
  46.7 12.1 %collective-permute-done.14.refs_3_ = s16[144,512]{1,0:T(8,128)(2,1)S(1)} collective-permute-done((s16[144,512]{1,0:T(8,128)(2,1)S(1)}, s16[144,512]{1,0:T(8,128)(2,1)S(1)}, u32[]{:S(2)}, u32[]{:S(2)}) %collective-permute-start.14) | collective-permute-done | bytes 147488 | tf_op jit(solution)/shard_map/ppermute | solution.py:235
  58.8 1.0 %finish.1 = bf16[256,512]{1,0:T(8,128)(2,1)} custom-call(f32[256,512]{1,0:T(8,128)S(1)} %get-tuple-element.43.kept, s16[272,512]{1,0:T(8,128)(2,1)S(1)} %collective-permute-done.7.coded, s16[144,512]{1,0:T(8,128)(2,1)S(1)} %collective-permute-done.9.refs_0_, s16[144,512]{1,0:T(8,128)(2,1)S(1)} %collective-permute-done.10.refs_1_, ...), custom_call_target="tpu_custom_call" | custom-call | tf_op jit(solution)/shard_map/finish/pallas_call | solution.py:209
  (21 shorter events, 3.5 us)
Async XLA Ops:
  0.0 5.9 %collective-permute-start.1 = (bf16[1536,1024]{1,0:T(8,128)(2,1)}, bf16[1536,1024]{1,0:T(8,128)(2,1)S(1)}, u32[]{:S(2)}, u32[]{:S(2)}) collective-permute-start(bf16[1536,1024]{1,0:T(8,128)(2,1)} %panels_in.1), channel_id=1, source_target_pairs={{0,1},{1,0},{2,3},{3,2},{4,5},{5,4},{6,7},{7,6},{8,9},{9,8},{10,11... | collective-permute-start | bytes 9437192 | tf_op jit(solution)/shard_map/ppermute | solution.py:235
  2.2 12.1 %collective-permute-start.3 = (bf16[128,1536]{1,0:T(8,128)(2,1)S(1)}, bf16[128,1536]{1,0:T(8,128)(2,1)S(1)}, u32[]{:S(2)}, u32[]{:S(2)}) collective-permute-start(bf16[128,1536]{1,0:T(8,128)(2,1)S(1)} %get-tuple-element.28.refs_0_), channel_id=1, source_target_pairs={{0,2},{1,3},{2,0},{3,1},{4,6},{5,7},{6,4},{7,5},{8,10},{9,11},{10,... | collective-permute-start | bytes 1179656 | tf_op jit(solution)/shard_map/ppermute | solution.py:235
  2.3 21.8 %collective-permute-start.6 = (bf16[128,1536]{1,0:T(8,128)(2,1)S(1)}, bf16[128,1536]{1,0:T(8,128)(2,1)S(1)}, u32[]{:S(2)}, u32[]{:S(2)}) collective-permute-start(bf16[128,1536]{1,0:T(8,128)(2,1)S(1)} %get-tuple-element.29.refs_1_), channel_id=1, source_target_pairs={{0,2},{1,3},{2,0},{3,1},{4,6},{5,7},{6,4},{7,5},{8,10},{9,11},{10,... | collective-permute-start | bytes 1179656 | tf_op jit(solution)/shard_map/ppermute | solution.py:235
  6.5 10.6 %collective-permute-start.2 = (s16[272,512]{1,0:T(8,128)(2,1)S(1)}, s16[272,512]{1,0:T(8,128)(2,1)S(1)}, u32[]{:S(2)}, u32[]{:S(2)}) collective-permute-start(s16[272,512]{1,0:T(8,128)(2,1)S(1)} %leaving.5), channel_id=1, source_target_pairs={{0,4},{1,5},{2,6},{3,7},{4,0},{5,1},{6,2},{7,3},{8,12},{9,13},{10,... | collective-permute-start | bytes 835592 | tf_op jit(solution)/shard_map/ppermute | solution.py:235
  8.1 14.0 %collective-permute-start = (s16[272,512]{1,0:T(8,128)(2,1)S(1)}, s16[272,512]{1,0:T(8,128)(2,1)S(1)}, u32[]{:S(2)}, u32[]{:S(2)}) collective-permute-start(s16[272,512]{1,0:T(8,128)(2,1)S(1)} %leaving.4), channel_id=1, source_target_pairs={{0,4},{1,5},{2,6},{3,7},{4,0},{5,1},{6,2},{7,3},{8,12},{9,13},{10,... | collective-permute-start | bytes 835592 | tf_op jit(solution)/shard_map/ppermute | solution.py:235
  15.0 13.1 %collective-permute-start.5 = (s16[272,512]{1,0:T(8,128)(2,1)S(1)}, s16[272,512]{1,0:T(8,128)(2,1)S(1)}, u32[]{:S(2)}, u32[]{:S(2)}) collective-permute-start(s16[272,512]{1,0:T(8,128)(2,1)S(1)} %leaving.6), channel_id=1, source_target_pairs={{0,4},{1,5},{2,6},{3,7},{4,0},{5,1},{6,2},{7,3},{8,12},{9,13},{10,... | collective-permute-start | bytes 835592 | tf_op jit(solution)/shard_map/ppermute | solution.py:235
  22.4 7.5 %collective-permute-start.4 = (s16[272,512]{1,0:T(8,128)(2,1)S(1)}, s16[272,512]{1,0:T(8,128)(2,1)S(1)}, u32[]{:S(2)}, u32[]{:S(2)}) collective-permute-start(s16[272,512]{1,0:T(8,128)(2,1)S(1)} %get-tuple-element.36), channel_id=1, source_target_pairs={{0,8},{1,9},{2,10},{3,11},{4,12},{5,13},{6,14},{7,15},{8,0},{9,1},... | collective-permute-start | bytes 835592 | tf_op jit(solution)/shard_map/ppermute | solution.py:235
  24.8 8.7 %collective-permute-start.11 = (s16[272,512]{1,0:T(8,128)(2,1)S(1)}, s16[272,512]{1,0:T(8,128)(2,1)S(1)}, u32[]{:S(2)}, u32[]{:S(2)}) collective-permute-start(s16[272,512]{1,0:T(8,128)(2,1)S(1)} %leaving.7), channel_id=1, source_target_pairs={{0,4},{1,5},{2,6},{3,7},{4,0},{5,1},{6,2},{7,3},{8,12},{9,13},{10,... | collective-permute-start | bytes 835592 | tf_op jit(solution)/shard_map/ppermute | solution.py:235
  28.2 5.2 %collective-permute-start.8 = (s16[144,512]{1,0:T(8,128)(2,1)S(1)}, s16[144,512]{1,0:T(8,128)(2,1)S(1)}, u32[]{:S(2)}, u32[]{:S(2)}) collective-permute-start(s16[144,512]{1,0:T(8,128)(2,1)S(1)} %get-tuple-element.40), channel_id=1, source_target_pairs={{0,8},{1,9},{2,10},{3,11},{4,12},{5,13},{6,14},{7,15},{8,0},{9,1},... | collective-permute-start | bytes 442376 | tf_op jit(solution)/shard_map/ppermute | solution.py:235
  33.8 6.7 %collective-permute-start.12 = (s16[144,512]{1,0:T(8,128)(2,1)S(1)}, s16[144,512]{1,0:T(8,128)(2,1)S(1)}, u32[]{:S(2)}, u32[]{:S(2)}) collective-permute-start(s16[144,512]{1,0:T(8,128)(2,1)S(1)} %get-tuple-element.48), channel_id=1, source_target_pairs={{0,8},{1,9},{2,10},{3,11},{4,12},{5,13},{6,14},{7,15},{8,0},{9,1},... | collective-permute-start | bytes 442376 | tf_op jit(solution)/shard_map/ppermute | solution.py:235
  35.4 10.0 %collective-permute-start.9 = (s16[144,512]{1,0:T(8,128)(2,1)S(1)}, s16[144,512]{1,0:T(8,128)(2,1)S(1)}, u32[]{:S(2)}, u32[]{:S(2)}) collective-permute-start(s16[144,512]{1,0:T(8,128)(2,1)S(1)} %merge.4), channel_id=1, source_target_pairs={{0,2},{1,3},{2,0},{3,1},{4,6},{5,7},{6,4},{7,5},{8,10},{9,11},{10,... | collective-permute-start | bytes 442376 | tf_op jit(solution)/shard_map/ppermute | solution.py:235
  35.9 10.8 %collective-permute-start.7 = (s16[272,512]{1,0:T(8,128)(2,1)S(1)}, s16[272,512]{1,0:T(8,128)(2,1)S(1)}, u32[]{:S(2)}, u32[]{:S(2)}) collective-permute-start(s16[272,512]{1,0:T(8,128)(2,1)S(1)} %get-tuple-element.44), channel_id=1, source_target_pairs={{2,18},{3,19},{6,22},{7,23},{10,26},{11,27},{14,30},{15,31},{16,0}... | collective-permute-start | bytes 835592 | tf_op jit(solution)/shard_map/ppermute | solution.py:235
  40.5 18.2 %collective-permute-start.14 = (s16[144,512]{1,0:T(8,128)(2,1)S(1)}, s16[144,512]{1,0:T(8,128)(2,1)S(1)}, u32[]{:S(2)}, u32[]{:S(2)}) collective-permute-start(s16[144,512]{1,0:T(8,128)(2,1)S(1)} %merge.5), channel_id=1, source_target_pairs={{2,16},{3,17},{6,20},{7,21},{10,24},{11,25},{14,28},{15,29},{16,2}... | collective-permute-start | bytes 442376 | tf_op jit(solution)/shard_map/ppermute | solution.py:235
  44.1 14.7 %collective-permute-start.13 = (s16[144,512]{1,0:T(8,128)(2,1)S(1)}, s16[144,512]{1,0:T(8,128)(2,1)S(1)}, u32[]{:S(2)}, u32[]{:S(2)}) collective-permute-start(s16[144,512]{1,0:T(8,128)(2,1)S(1)} %merge.5), channel_id=1, source_target_pairs={{0,2},{1,3},{4,6},{5,7},{8,10},{9,11},{12,14},{13,15},{18,16},{19,... | collective-permute-start | bytes 442376 | tf_op jit(solution)/shard_map/ppermute | solution.py:235
  45.4 13.4 %collective-permute-start.10 = (s16[144,512]{1,0:T(8,128)(2,1)S(1)}, s16[144,512]{1,0:T(8,128)(2,1)S(1)}, u32[]{:S(2)}, u32[]{:S(2)}) collective-permute-start(s16[144,512]{1,0:T(8,128)(2,1)S(1)} %collective-permute-done.9.refs_0_), channel_id=1, source_target_pairs={{0,16},{1,17},{4,20},{5,21},{8,24},{9,25},{12,28},{13,29},{18,2},{... | collective-permute-start | bytes 442376 | tf_op jit(solution)/shard_map/ppermute | solution.py:235

commit v2 on v1

--- a/solution.py
+++ b/solution.py
@@ -216,6 +216,81 @@
     )(kept, coded, *parts)
 
 
+def chosen_kernel(block, *refs, coded, spread):
+    panels, out = refs[:-1], refs[-1]
+    width = out.shape[1]
+    step = min(width, 256)
+    stays = places(spread)[1]
+    for k, panel in enumerate(panels):
+
+        @pl.when(stays == (1 - k if coded else k))
+        def _():
+            for n in range(0, width, step):
+                at = slice(n, n + step)
+                value = jnp.dot(block[...], panel[:, at], preferred_element_type=jnp.float32)
+                if coded:
+                    encode(value, out, at)
+                else:
+                    out[:, at] = value
+
+
+def chosen(block, panels, spread, coded):
+    height, width = block.shape[0], panels[0].shape[1]
+    return pl.pallas_call(
+        functools.partial(chosen_kernel, coded=coded, spread=spread),
+        out_shape=coded_shape(height, width) if coded else jax.ShapeDtypeStruct((height, width), jnp.float32),
+        in_specs=[VMEM] * 3,
+        out_specs=VMEM,
+        compiler_params=SMALL,
+        name="chosen",
+    )(block, *panels)
+
+
+def halve_kernel(coded, kept, hold, send, *, spread):
+    height, half = hold.shape
+    side = places(spread)[0]
+
+    def value(which):
+        at = pl.ds(pl.multiple_of(which * half, half), half)
+        return kept[:, at] + decode(coded[:, at], height)
+
+    encode(value(1 - side), send)
+    hold[...] = value(side)
+
+
+def halve(coded, kept, spread):
+    height, half = kept.shape[0], kept.shape[1] // spread
+    return pl.pallas_call(
+        functools.partial(halve_kernel, spread=spread),
+        out_shape=[jax.ShapeDtypeStruct((height, half), jnp.float32), coded_shape(height, half)],
+        in_specs=[VMEM, VMEM],
+        out_specs=[VMEM, VMEM],
+        compiler_params=SMALL,
+        name="halve",
+    )(coded, kept)
+
+
+def join_kernel(*refs):
+    count = (len(refs) - 2) // 2
+    value = jnp.concatenate(
+        [kept[...] + decode(coded[...], kept.shape[0]) for coded, kept in zip(refs[:count], refs[count:-2])], 0
+    )
+    refs[-2][...] = value
+    encode(value, refs[-1])
+
+
+def join(codeds, kepts):
+    height, half = sum(kept.shape[0] for kept in kepts), kepts[0].shape[1]
+    return pl.pallas_call(
+        join_kernel,
+        out_shape=[jax.ShapeDtypeStruct((height, half), jnp.float32), coded_shape(height, half)],
+        in_specs=[VMEM] * (2 * len(kepts)),
+        out_specs=[VMEM, VMEM],
+        compiler_params=SMALL,
+        name="join",
+    )(*codeds, *kepts)
+
+
 def after(value, *others):
     return lax.optimization_barrier((value, *others))[0]
 
@@ -275,45 +350,63 @@
             bit //= 2
         moved = [m for m in sorted(dense) if m]
 
-        first = products(own, [panels], half, True)
-        sent = [across(first)]
-        second = products(own, [after(other, first)], half, True)
-        sent.append(across(second))
-        kept = products(own, [after(panels, second), other], half, False)
+        both = [panels, other]
+        code_a = products(own[:1], both, half, True)
+        got_a = across(code_a)
+        order = code_a
+        gots_b, stays_b = [], []
+        for block in own[1:]:
+            order = chosen(after(block, order), both, spread, True)
+            gots_b.append(along(order))
+        stay_a = products([after(own[0], order)], both, half, False)
+        order = stay_a
+        for block in own[1:]:
+            order = chosen(after(block, order), both, spread, False)
+            stays_b.append(order)
         coded, stay = {}, {}
 
-        def multiply(j, order):
+        def leave(j, order):
             for m in moved:
-                block = after(dense[m][j], order)
-                code = products([block], [panels, other], half, True)
-                coded[m, j] = across(code)
-                stay[m, j] = products([after(block, code)], [panels, other], half, False)
-
-        multiply(0, kept)
-        hold, send = split([sent[0], after(sent[1], stay[moved[0], 0])], kept, spread)
-        got = along(send)
+                order = products([after(dense[m][j], order)], both, half, True)
+                coded[m, j] = across(order)
+            return order
+
+        def keep(j, order):
+            for m in moved:
+                order = stay[m, j] = products([after(dense[m][j], order)], both, half, False)
+            return order
+
+        order = leave(0, order)
+        hold, send = split([after(got_a, order)], stay_a, spread)
+        holds, gots, order = [hold], [along(send)], send
+        for got_b, stay_b in zip(gots_b, stays_b):
+            hold, send = halve(after(got_b, order), stay_b, spread)
+            holds.append(hold)
+            gots.append(across(send))
+            order = send
+        order = keep(0, order)
+        hold, send = join([after(gots[0], order), *gots[1:]], holds)
+        bit = 2
+        while bit < last:
+            got = permute(
+                send,
+                lambda r, c: (r ^ (bit * spread), c) if met(r, c, bit - 2) and not met(r, c, bit) else None,
+            )
+            hold, send = merge(got, hold, 1)
+            bit *= 2
+        got = permute(send, lambda r, c: (r ^ (last * spread), c) if met(r, c, inner) and not met(r, c, last) else None)
+        order = send
         for j in range(1, chunks):
-            multiply(j, send)
+            order = keep(j, leave(j, order))
 
         parts = {}
-        order = stay[moved[-1], chunks - 1]
         for j in range(chunks):
             for m in moved:
-                part_hold, part_send = split([after(coded[m, j], order)], stay[m, j], spread)
-                part_got, part_hold = folded(along(part_send), part_hold)
-                if j == 0 and m == moved[0]:
-                    got, hold = folded(got, hold)
-                    hold, send = merge(after(got, part_send), hold, 1)
-                    got = permute(
-                        send,
-                        lambda r, c: (r ^ (last * spread), c)
-                        if met(r, c, inner) and not met(r, c, last)
-                        else None,
-                    )
-                _, code = merge(after(part_got, send), part_hold, 0)
-                order = code
+                part_hold, order = split([after(coded[m, j], order)], stay[m, j], spread)
+                part_got, part_hold = folded(along(order), part_hold)
+                _, order = merge(part_got, part_hold, 0)
                 if j == 0:
-                    near = permute(code, lambda r, c: (r, c ^ m) if met(r, c, inner) else None)
+                    near = permute(order, lambda r, c: (r, c ^ m) if met(r, c, inner) else None)
                     far = permute(
                         near,
                         lambda r, c: (r ^ (last * spread), c)
@@ -322,12 +415,12 @@
                     )
                 else:
                     far = permute(
-                        code,
+                        order,
                         lambda r, c: (r ^ (last * spread), c ^ m)
                         if met(r, c, inner) and not met(r, c, last)
                         else None,
                     )
-                    near = permute(code, lambda r, c: (r, c ^ m) if met(r, c, inner | last) else None)
+                    near = permute(order, lambda r, c: (r, c ^ m) if met(r, c, inner | last) else None)
                 parts[m, j] = [near, far]
         pieces = [x for m in moved for j in range(chunks) for x in parts[m, j]]
         return finish(hold, got, pieces, chunks, spread)

time: 59.9 us -> 59.4 us (level)
  the two profiles are of different devices: /device:TPU:4 before, /device:TPU:0 now
where the time goes in v2:
time: 59.4 us; the launch traced here: 59.2 us
  starting transfers between devices  30.6 us (52%)
  waiting for transfers between devices  18.8 us (32%)
  Pallas kernels  9.62 us (16%)
    ppermute x16, starting transfers between devices, permute(): return lax.ppermute(value, ('row', 'col'), pairs)  30.6 us
    ppermute x16, waiting for transfers between devices, permute(): return lax.ppermute(value, ('row', 'col'), pairs)  18.8 us
    pallas_call x6, Pallas kernels, products(): pl.pallas_call(functools.partial(product_kernel, count=len(blocks), coded...  4.15 us
    pallas_call x1, Pallas kernels, build(): pl.pallas_call(build_kernel, out_shape=[jax.ShapeDtypeStruct((edge, tall...  2.17 us
    pallas_call x2, Pallas kernels, chosen(): pl.pallas_call(functools.partial(chosen_kernel, coded=coded, spread=sprea...  1.28 us
  transfers between devices with their start and end apart: 16, of which 8 were waited for; matrix products, arithmetic and copies ran while one was open for 0% of the time, Pallas kernels for 15%

profile of v2, /device:TPU:0, one launch (start us, length us, event | category | flops | bytes accessed | tf_op | source)
XLA Modules:
  0.0 59.2 jit_solution(594528161232202928)
XLA Ops:
  0.5 2.2 %build.1 = (bf16[128,1536]{1,0:T(8,128)(2,1)S(1)}, bf16[128,1536]{1,0:T(8,128)(2,1)S(1)}, bf16[1536,1024]{1,0:T(8,128)(2,1)S(1)}) custom-call(s32[12]{0:T(128)} %bitcast.2, s32[24]{0:T(128)} %bitcast.3, bf16[24,128,128]{2,1,0:T(8,128)(2,1)} %tiles_in.1, bf16[1536,1024]{1,0:T(8,128)(2,1)} %panels_in.1), custom_call_target="tpu_custom_call" | custom-call | tf_op jit(solution)/shard_map/build/pallas_call | solution.py:93
  2.7 2.6 %collective-permute-start.2 = (bf16[128,1536]{1,0:T(8,128)(2,1)S(1)}, bf16[128,1536]{1,0:T(8,128)(2,1)S(1)}, u32[]{:S(2)}, u32[]{:S(2)}) collective-permute-start(bf16[128,1536]{1,0:T(8,128)(2,1)S(1)} %get-tuple-element.34.refs_0_), channel_id=1, source_target_pairs={{0,2},{1,3},{2,0},{3,1},{4,6},{5,7},{6,4},{7,5},{8,10},{9,11},{10,... | collective-permute-start | bytes 1179656 | tf_op jit(solution)/shard_map/ppermute | solution.py:310
  5.2 0.7 %collective-permute-done.refs_2_.refs_1_ = bf16[1536,1024]{1,0:T(8,128)(2,1)S(1)} collective-permute-done((bf16[1536,1024]{1,0:T(8,128)(2,1)}, bf16[1536,1024]{1,0:T(8,128)(2,1)S(1)}, u32[]{:S(2)}, u32[]{:S(2)}) %collective-permute-start) | collective-permute-done | bytes 3145760 | tf_op jit(solution)/shard_map/ppermute | solution.py:310
  6.0 0.8 %leaving.3 = s16[272,512]{1,0:T(8,128)(2,1)S(1)} custom-call(bf16[128,1536]{1,0:T(8,128)(2,1)S(1)} %get-tuple-element.34.refs_0_, bf16[1536,1024]{1,0:T(8,128)(2,1)S(1)} %get-tuple-element.31.refs_1_.refs_0_, bf16[1536,1024]{1,0:T(8,128)(2,1)S(1)} %collective-permute-done.refs_2_.refs_1_), custom_call_target="tpu_custom_call" | custom-call | tf_op jit(solution)/shard_map/leaving/pallas_call | solution.py:134
  7.4 3.0 %collective-permute-start.4 = (s16[144,1024]{1,0:T(8,128)(2,1)S(1)}, s16[144,1024]{1,0:T(8,128)(2,1)S(1)}, u32[]{:S(2)}, u32[]{:S(2)}) collective-permute-start(s16[144,1024]{1,0:T(8,128)(2,1)S(1)} %chosen.2), channel_id=1, source_target_pairs={{0,8},{1,9},{2,10},{3,11},{4,12},{5,13},{6,14},{7,15},{8,0},{9,1},... | collective-permute-start | bytes 884744 | tf_op jit(solution)/shard_map/ppermute | solution.py:310
  10.4 1.5 %collective-permute-start.1 = (s16[272,512]{1,0:T(8,128)(2,1)S(1)}, s16[272,512]{1,0:T(8,128)(2,1)S(1)}, u32[]{:S(2)}, u32[]{:S(2)}) collective-permute-start(s16[272,512]{1,0:T(8,128)(2,1)S(1)} %leaving.3), channel_id=1, source_target_pairs={{0,4},{1,5},{2,6},{3,7},{4,0},{5,1},{6,2},{7,3},{8,12},{9,13},{10,... | collective-permute-start | bytes 835592 | tf_op jit(solution)/shard_map/ppermute | solution.py:310
  11.9 1.5 %collective-permute-start.8 = (bf16[128,1536]{1,0:T(8,128)(2,1)S(1)}, bf16[128,1536]{1,0:T(8,128)(2,1)S(1)}, u32[]{:S(2)}, u32[]{:S(2)}) collective-permute-start(bf16[128,1536]{1,0:T(8,128)(2,1)S(1)} %get-tuple-element.35.block), channel_id=1, source_target_pairs={{0,2},{1,3},{2,0},{3,1},{4,6},{5,7},{6,4},{7,5},{8,10},{9,11},{10,... | collective-permute-start | bytes 1179656 | tf_op jit(solution)/shard_map/ppermute | solution.py:310
  15.2 0.8 %leaving.4 = s16[272,512]{1,0:T(8,128)(2,1)S(1)} custom-call(bf16[128,1536]{1,0:T(8,128)(2,1)S(1)} %collective-permute-done.2.refs_0_, bf16[1536,1024]{1,0:T(8,128)(2,1)S(1)} %get-tuple-element.31.refs_1_.refs_0_, bf16[1536,1024]{1,0:T(8,128)(2,1)S(1)} %collective-permute-done.refs_2_.refs_1_), custom_call_target="tpu_custom_call" | custom-call | tf_op jit(solution)/shard_map/leaving/pallas_call | solution.py:134
  16.0 2.9 %collective-permute-done.1.refs_0_ = s16[272,512]{1,0:T(8,128)(2,1)S(1)} collective-permute-done((s16[272,512]{1,0:T(8,128)(2,1)S(1)}, s16[272,512]{1,0:T(8,128)(2,1)S(1)}, u32[]{:S(2)}, u32[]{:S(2)}) %collective-permute-start.1) | collective-permute-done | bytes 278560 | tf_op jit(solution)/shard_map/ppermute | solution.py:310
  19.6 1.6 %collective-permute-start.5 = (s16[144,512]{1,0:T(8,128)(2,1)S(1)}, s16[144,512]{1,0:T(8,128)(2,1)S(1)}, u32[]{:S(2)}, u32[]{:S(2)}) collective-permute-start(s16[144,512]{1,0:T(8,128)(2,1)S(1)} %get-tuple-element.40), channel_id=1, source_target_pairs={{0,4},{1,5},{2,6},{3,7},{4,0},{5,1},{6,2},{7,3},{8,12},{9,13},{10,... | collective-permute-start | bytes 442376 | tf_op jit(solution)/shard_map/ppermute | solution.py:310
  22.4 1.9 %collective-permute-done.3.refs_0_ = s16[144,512]{1,0:T(8,128)(2,1)S(1)} collective-permute-done((s16[144,512]{1,0:T(8,128)(2,1)S(1)}, s16[144,512]{1,0:T(8,128)(2,1)S(1)}, u32[]{:S(2)}, u32[]{:S(2)}) %collective-permute-start.3) | collective-permute-done | bytes 147488 | tf_op jit(solution)/shard_map/ppermute | solution.py:310
  24.2 2.2 %collective-permute-done.5.refs_1_ = s16[144,512]{1,0:T(8,128)(2,1)S(1)} collective-permute-done((s16[144,512]{1,0:T(8,128)(2,1)S(1)}, s16[144,512]{1,0:T(8,128)(2,1)S(1)}, u32[]{:S(2)}, u32[]{:S(2)}) %collective-permute-start.5) | collective-permute-done | bytes 147488 | tf_op jit(solution)/shard_map/ppermute | solution.py:310
  26.6 0.8 %leaving.5 = s16[272,512]{1,0:T(8,128)(2,1)S(1)} custom-call(bf16[128,1536]{1,0:T(8,128)(2,1)S(1)} %collective-permute-done.8.refs_0_, bf16[1536,1024]{1,0:T(8,128)(2,1)S(1)} %get-tuple-element.31.refs_1_.refs_0_, bf16[1536,1024]{1,0:T(8,128)(2,1)S(1)} %collective-permute-done.refs_2_.refs_1_), custom_call_target="tpu_custom_call" | custom-call | tf_op jit(solution)/shard_map/leaving/pallas_call | solution.py:134
  27.4 1.6 %collective-permute-start.12 = (s16[272,512]{1,0:T(8,128)(2,1)S(1)}, s16[272,512]{1,0:T(8,128)(2,1)S(1)}, u32[]{:S(2)}, u32[]{:S(2)}) collective-permute-start(s16[272,512]{1,0:T(8,128)(2,1)S(1)} %leaving.5), channel_id=1, source_target_pairs={{0,4},{1,5},{2,6},{3,7},{4,0},{5,1},{6,2},{7,3},{8,12},{9,13},{10,... | collective-permute-start | bytes 835592 | tf_op jit(solution)/shard_map/ppermute | solution.py:310
  29.7 2.7 %collective-permute-done.7.refs_0_ = s16[272,512]{1,0:T(8,128)(2,1)S(1)} collective-permute-done((s16[272,512]{1,0:T(8,128)(2,1)S(1)}, s16[272,512]{1,0:T(8,128)(2,1)S(1)}, u32[]{:S(2)}, u32[]{:S(2)}) %collective-permute-start.7) | collective-permute-done | bytes 278560 | tf_op jit(solution)/shard_map/ppermute | solution.py:310
  32.5 1.7 %collective-permute-start.9 = (s16[144,512]{1,0:T(8,128)(2,1)S(1)}, s16[144,512]{1,0:T(8,128)(2,1)S(1)}, u32[]{:S(2)}, u32[]{:S(2)}) collective-permute-start(s16[144,512]{1,0:T(8,128)(2,1)S(1)} %get-tuple-element.50), channel_id=1, source_target_pairs={{0,8},{1,9},{2,10},{3,11},{4,12},{5,13},{6,14},{7,15},{8,0},{9,1},... | collective-permute-start | bytes 442376 | tf_op jit(solution)/shard_map/ppermute | solution.py:310
  34.3 3.9 %collective-permute-done.9.coded = s16[144,512]{1,0:T(8,128)(2,1)S(1)} collective-permute-done((s16[144,512]{1,0:T(8,128)(2,1)S(1)}, s16[144,512]{1,0:T(8,128)(2,1)S(1)}, u32[]{:S(2)}, u32[]{:S(2)}) %collective-permute-start.9) | collective-permute-done | bytes 147488 | tf_op jit(solution)/shard_map/ppermute | solution.py:310
  38.3 2.2 %collective-permute-start.10 = (s16[144,512]{1,0:T(8,128)(2,1)S(1)}, s16[144,512]{1,0:T(8,128)(2,1)S(1)}, u32[]{:S(2)}, u32[]{:S(2)}) collective-permute-start(s16[144,512]{1,0:T(8,128)(2,1)S(1)} %merge.2), channel_id=1, source_target_pairs={{0,2},{1,3},{2,0},{3,1},{4,6},{5,7},{6,4},{7,5},{8,10},{9,11},{10,... | collective-permute-start | bytes 442376 | tf_op jit(solution)/shard_map/ppermute | solution.py:310
  40.7 1.6 %collective-permute-start.13 = (s16[144,512]{1,0:T(8,128)(2,1)S(1)}, s16[144,512]{1,0:T(8,128)(2,1)S(1)}, u32[]{:S(2)}, u32[]{:S(2)}) collective-permute-start(s16[144,512]{1,0:T(8,128)(2,1)S(1)} %get-tuple-element.53), channel_id=1, source_target_pairs={{0,8},{1,9},{2,10},{3,11},{4,12},{5,13},{6,14},{7,15},{8,0},{9,1},... | collective-permute-start | bytes 442376 | tf_op jit(solution)/shard_map/ppermute | solution.py:310
  42.3 1.3 %collective-permute-start.6 = (s16[272,512]{1,0:T(8,128)(2,1)S(1)}, s16[272,512]{1,0:T(8,128)(2,1)S(1)}, u32[]{:S(2)}, u32[]{:S(2)}) collective-permute-start(s16[272,512]{1,0:T(8,128)(2,1)S(1)} %get-tuple-element.46), channel_id=1, source_target_pairs={{2,18},{3,19},{6,22},{7,23},{10,26},{11,27},{14,30},{15,31},{16,0}... | collective-permute-start | bytes 835592 | tf_op jit(solution)/shard_map/ppermute | solution.py:310
  43.6 5.4 %collective-permute-start.11 = (s16[144,512]{1,0:T(8,128)(2,1)S(1)}, s16[144,512]{1,0:T(8,128)(2,1)S(1)}, u32[]{:S(2)}, u32[]{:S(2)}) collective-permute-start(s16[144,512]{1,0:T(8,128)(2,1)S(1)} %collective-permute-done.10.refs_0_), channel_id=1, source_target_pairs={{0,16},{1,17},{4,20},{5,21},{8,24},{9,25},{12,28},{13,29},{18,2},{... | collective-permute-start | bytes 442376 | tf_op jit(solution)/shard_map/ppermute | solution.py:310
  49.9 4.4 %collective-permute-start.14 = (s16[144,512]{1,0:T(8,128)(2,1)S(1)}, s16[144,512]{1,0:T(8,128)(2,1)S(1)}, u32[]{:S(2)}, u32[]{:S(2)}) collective-permute-start(s16[144,512]{1,0:T(8,128)(2,1)S(1)} %merge.3), channel_id=1, source_target_pairs={{0,2},{1,3},{4,6},{5,7},{8,10},{9,11},{12,14},{13,15},{18,16},{19,... | collective-permute-start | bytes 442376 | tf_op jit(solution)/shard_map/ppermute | solution.py:310
  54.2 4.0 %collective-permute-done.6.coded = s16[272,512]{1,0:T(8,128)(2,1)S(1)} collective-permute-done((s16[272,512]{1,0:T(8,128)(2,1)S(1)}, s16[272,512]{1,0:T(8,128)(2,1)S(1)}, u32[]{:S(2)}, u32[]{:S(2)}) %collective-permute-start.6) | collective-permute-done | bytes 278560 | tf_op jit(solution)/shard_map/ppermute | solution.py:310
  58.2 1.0 %finish.1 = bf16[256,512]{1,0:T(8,128)(2,1)} custom-call(f32[256,512]{1,0:T(8,128)S(1)} %get-tuple-element.45.kept, s16[272,512]{1,0:T(8,128)(2,1)S(1)} %collective-permute-done.6.coded, s16[144,512]{1,0:T(8,128)(2,1)S(1)} %collective-permute-done.10.refs_0_, s16[144,512]{1,0:T(8,128)(2,1)S(1)} %collective-permute-done.11.refs_1_, ...), custom_call_target="tpu_custom_call" | custom-call | tf_op jit(solution)/shard_map/finish/pallas_call | solution.py:209
  (25 shorter events, 6.8 us)
Async XLA Ops:
  0.0 6.0 %collective-permute-start = (bf16[1536,1024]{1,0:T(8,128)(2,1)}, bf16[1536,1024]{1,0:T(8,128)(2,1)S(1)}, u32[]{:S(2)}, u32[]{:S(2)}) collective-permute-start(bf16[1536,1024]{1,0:T(8,128)(2,1)} %panels_in.1), channel_id=1, source_target_pairs={{0,1},{1,0},{2,3},{3,2},{4,5},{5,4},{6,7},{7,6},{8,9},{9,8},{10,11... | collective-permute-start | bytes 9437192 | tf_op jit(solution)/shard_map/ppermute | solution.py:310
  2.7 12.5 %collective-permute-start.2 = (bf16[128,1536]{1,0:T(8,128)(2,1)S(1)}, bf16[128,1536]{1,0:T(8,128)(2,1)S(1)}, u32[]{:S(2)}, u32[]{:S(2)}) collective-permute-start(bf16[128,1536]{1,0:T(8,128)(2,1)S(1)} %get-tuple-element.34.refs_0_), channel_id=1, source_target_pairs={{0,2},{1,3},{2,0},{3,1},{4,6},{5,7},{6,4},{7,5},{8,10},{9,11},{10,... | collective-permute-start | bytes 1179656 | tf_op jit(solution)/shard_map/ppermute | solution.py:310
  7.4 12.0 %collective-permute-start.4 = (s16[144,1024]{1,0:T(8,128)(2,1)S(1)}, s16[144,1024]{1,0:T(8,128)(2,1)S(1)}, u32[]{:S(2)}, u32[]{:S(2)}) collective-permute-start(s16[144,1024]{1,0:T(8,128)(2,1)S(1)} %chosen.2), channel_id=1, source_target_pairs={{0,8},{1,9},{2,10},{3,11},{4,12},{5,13},{6,14},{7,15},{8,0},{9,1},... | collective-permute-start | bytes 884744 | tf_op jit(solution)/shard_map/ppermute | solution.py:310
  10.4 8.4 %collective-permute-start.1 = (s16[272,512]{1,0:T(8,128)(2,1)S(1)}, s16[272,512]{1,0:T(8,128)(2,1)S(1)}, u32[]{:S(2)}, u32[]{:S(2)}) collective-permute-start(s16[272,512]{1,0:T(8,128)(2,1)S(1)} %leaving.3), channel_id=1, source_target_pairs={{0,4},{1,5},{2,6},{3,7},{4,0},{5,1},{6,2},{7,3},{8,12},{9,13},{10,... | collective-permute-start | bytes 835592 | tf_op jit(solution)/shard_map/ppermute | solution.py:310
  11.9 14.7 %collective-permute-start.8 = (bf16[128,1536]{1,0:T(8,128)(2,1)S(1)}, bf16[128,1536]{1,0:T(8,128)(2,1)S(1)}, u32[]{:S(2)}, u32[]{:S(2)}) collective-permute-start(bf16[128,1536]{1,0:T(8,128)(2,1)S(1)} %get-tuple-element.35.block), channel_id=1, source_target_pairs={{0,2},{1,3},{2,0},{3,1},{4,6},{5,7},{6,4},{7,5},{8,10},{9,11},{10,... | collective-permute-start | bytes 1179656 | tf_op jit(solution)/shard_map/ppermute | solution.py:310
  19.0 5.2 %collective-permute-start.3 = (s16[144,512]{1,0:T(8,128)(2,1)S(1)}, s16[144,512]{1,0:T(8,128)(2,1)S(1)}, u32[]{:S(2)}, u32[]{:S(2)}) collective-permute-start(s16[144,512]{1,0:T(8,128)(2,1)S(1)} %get-tuple-element.38), channel_id=1, source_target_pairs={{0,8},{1,9},{2,10},{3,11},{4,12},{5,13},{6,14},{7,15},{8,0},{9,1},... | collective-permute-start | bytes 442376 | tf_op jit(solution)/shard_map/ppermute | solution.py:310
  19.6 6.8 %collective-permute-start.5 = (s16[144,512]{1,0:T(8,128)(2,1)S(1)}, s16[144,512]{1,0:T(8,128)(2,1)S(1)}, u32[]{:S(2)}, u32[]{:S(2)}) collective-permute-start(s16[144,512]{1,0:T(8,128)(2,1)S(1)} %get-tuple-element.40), channel_id=1, source_target_pairs={{0,4},{1,5},{2,6},{3,7},{4,0},{5,1},{6,2},{7,3},{8,12},{9,13},{10,... | collective-permute-start | bytes 442376 | tf_op jit(solution)/shard_map/ppermute | solution.py:310
  21.3 11.1 %collective-permute-start.7 = (s16[272,512]{1,0:T(8,128)(2,1)S(1)}, s16[272,512]{1,0:T(8,128)(2,1)S(1)}, u32[]{:S(2)}, u32[]{:S(2)}) collective-permute-start(s16[272,512]{1,0:T(8,128)(2,1)S(1)} %leaving.4), channel_id=1, source_target_pairs={{0,4},{1,5},{2,6},{3,7},{4,0},{5,1},{6,2},{7,3},{8,12},{9,13},{10,... | collective-permute-start | bytes 835592 | tf_op jit(solution)/shard_map/ppermute | solution.py:310
  27.4 13.1 %collective-permute-start.12 = (s16[272,512]{1,0:T(8,128)(2,1)S(1)}, s16[272,512]{1,0:T(8,128)(2,1)S(1)}, u32[]{:S(2)}, u32[]{:S(2)}) collective-permute-start(s16[272,512]{1,0:T(8,128)(2,1)S(1)} %leaving.5), channel_id=1, source_target_pairs={{0,4},{1,5},{2,6},{3,7},{4,0},{5,1},{6,2},{7,3},{8,12},{9,13},{10,... | collective-permute-start | bytes 835592 | tf_op jit(solution)/shard_map/ppermute | solution.py:310
  32.5 5.6 %collective-permute-start.9 = (s16[144,512]{1,0:T(8,128)(2,1)S(1)}, s16[144,512]{1,0:T(8,128)(2,1)S(1)}, u32[]{:S(2)}, u32[]{:S(2)}) collective-permute-start(s16[144,512]{1,0:T(8,128)(2,1)S(1)} %get-tuple-element.50), channel_id=1, source_target_pairs={{0,8},{1,9},{2,10},{3,11},{4,12},{5,13},{6,14},{7,15},{8,0},{9,1},... | collective-permute-start | bytes 442376 | tf_op jit(solution)/shard_map/ppermute | solution.py:310
  38.3 5.4 %collective-permute-start.10 = (s16[144,512]{1,0:T(8,128)(2,1)S(1)}, s16[144,512]{1,0:T(8,128)(2,1)S(1)}, u32[]{:S(2)}, u32[]{:S(2)}) collective-permute-start(s16[144,512]{1,0:T(8,128)(2,1)S(1)} %merge.2), channel_id=1, source_target_pairs={{0,2},{1,3},{2,0},{3,1},{4,6},{5,7},{6,4},{7,5},{8,10},{9,11},{10,... | collective-permute-start | bytes 442376 | tf_op jit(solution)/shard_map/ppermute | solution.py:310
  40.7 8.4 %collective-permute-start.13 = (s16[144,512]{1,0:T(8,128)(2,1)S(1)}, s16[144,512]{1,0:T(8,128)(2,1)S(1)}, u32[]{:S(2)}, u32[]{:S(2)}) collective-permute-start(s16[144,512]{1,0:T(8,128)(2,1)S(1)} %get-tuple-element.53), channel_id=1, source_target_pairs={{0,8},{1,9},{2,10},{3,11},{4,12},{5,13},{6,14},{7,15},{8,0},{9,1},... | collective-permute-start | bytes 442376 | tf_op jit(solution)/shard_map/ppermute | solution.py:310
  42.3 16.0 %collective-permute-start.6 = (s16[272,512]{1,0:T(8,128)(2,1)S(1)}, s16[272,512]{1,0:T(8,128)(2,1)S(1)}, u32[]{:S(2)}, u32[]{:S(2)}) collective-permute-start(s16[272,512]{1,0:T(8,128)(2,1)S(1)} %get-tuple-element.46), channel_id=1, source_target_pairs={{2,18},{3,19},{6,22},{7,23},{10,26},{11,27},{14,30},{15,31},{16,0}... | collective-permute-start | bytes 835592 | tf_op jit(solution)/shard_map/ppermute | solution.py:310
  43.6 14.6 %collective-permute-start.11 = (s16[144,512]{1,0:T(8,128)(2,1)S(1)}, s16[144,512]{1,0:T(8,128)(2,1)S(1)}, u32[]{:S(2)}, u32[]{:S(2)}) collective-permute-start(s16[144,512]{1,0:T(8,128)(2,1)S(1)} %collective-permute-done.10.refs_0_), channel_id=1, source_target_pairs={{0,16},{1,17},{4,20},{5,21},{8,24},{9,25},{12,28},{13,29},{18,2},{... | collective-permute-start | bytes 442376 | tf_op jit(solution)/shard_map/ppermute | solution.py:310
  49.2 9.1 %collective-permute-start.15 = (s16[144,512]{1,0:T(8,128)(2,1)S(1)}, s16[144,512]{1,0:T(8,128)(2,1)S(1)}, u32[]{:S(2)}, u32[]{:S(2)}) collective-permute-start(s16[144,512]{1,0:T(8,128)(2,1)S(1)} %merge.3), channel_id=1, source_target_pairs={{2,16},{3,17},{6,20},{7,21},{10,24},{11,25},{14,28},{15,29},{16,2}... | collective-permute-start | bytes 442376 | tf_op jit(solution)/shard_map/ppermute | solution.py:310
  49.9 8.4 %collective-permute-start.14 = (s16[144,512]{1,0:T(8,128)(2,1)S(1)}, s16[144,512]{1,0:T(8,128)(2,1)S(1)}, u32[]{:S(2)}, u32[]{:S(2)}) collective-permute-start(s16[144,512]{1,0:T(8,128)(2,1)S(1)} %merge.3), channel_id=1, source_target_pairs={{0,2},{1,3},{4,6},{5,7},{8,10},{9,11},{12,14},{13,15},{18,16},{19,... | collective-permute-start | bytes 442376 | tf_op jit(solution)/shard_map/ppermute | solution.py:310
